TPU v7x, 32 devices: a whole 2x2x4 slice. The times are simulated.
32 devices in a mesh: member: 4 (over y, x), space: 8 (over z, core).
Axes of the slice: x: 2, y: 2, z: 4, core: 2. Of those that a mesh axis runs over, the one named last changes fastest.
Arguments:
- ensemble: float32 [128, 16, 16, 128], P(None, 'space', 'member'), may hold values from -4 to 4
- source: float32 [16, 16, 128], P('space', 'member'), may hold values from -6 to 6
- obs_rows: int32 [8, 4, 1], P('space', 'member'), may hold values from 0 to 7
- obs_values: float32 [8, 4, 128], P('space', 'member'), may hold values from -3 to 3
- obs_noise: float32 [128, 8, 4, 128], P(None, 'space', 'member'), may hold values from -5 to 5
- obs_var: float32 [8, 4, 128], P('space', 'member'), may hold values from 0.05 to 2
Outputs:
- updated: float32 [128, 16, 16, 128], P(None, 'space', 'member')
- predicted: float32 [128, 8, 4, 128], P(None, 'space', 'member')
Inputs may be any that keep to these rules, and one draw needn't show every extreme that they name: `obs_rows`: entry [s, m, o] names the cell row at (s * 2 + r // 4, m * 4 + r % 4) of the first two dimensions, whose 128 cells along the third dimension are observed; rows may repeat.
All inputs are finite; a program needn't handle non-finite values.
Results may differ from a plain program's by a relative error of at most 0.0003.
Values sent between devices are 32-bit elements; how exact they have to be, the bound alone decides.
No kernel may reach another device: no remote copies, remote signals or barrier semaphores. Data moves between devices by JAX's collectives and lax.ppermute only.
A program may use at most 64 MiB of HBM per device.

v0:
```python
import jax
import jax.numpy as jnp
from jax import lax
from jax.sharding import PartitionSpec as P

ITERS = 4


def padded_2(x, sides, width):
    for axis, dim in sides:
        devices, length = (lax.axis_size(axis), x.shape[dim])
        up = [(i, (i + 1) % devices) for i in range(devices - 1)]
        down = [(j, i) for i, j in up]
        last = lax.slice_in_dim(x, length - width, length, axis=dim)
        leading = lax.slice_in_dim(x, 0, width, axis=dim)
        before = lax.ppermute(last, axis, up)
        after = lax.ppermute(leading, axis, down)
        x = jnp.concatenate([before, x, after], axis=dim)
    return x


def harmonic(first_cond, second_cond):
    return 2.0 * first_cond * second_cond / (first_cond + second_cond)


def extend_cond(cond):
    widened = padded_2(cond, (("member", 2),), 1)
    return jnp.pad(widened, ((0, 0), (1, 1), (0, 0), (1, 1)))


def extend_values(values_in):
    widened = padded_2(values_in, (("member", 2),), 1)
    return jnp.pad(widened, ((0, 0), (1, 1), (0, 0), (1, 1)))


def member_dots(dot_terms):
    return lax.psum(dot_terms, "member")


def face_terms(cond):
    widened = extend_cond(cond)
    edge_pad = jnp.pad(cond, ((0, 0), (1, 1), (1, 1), (1, 1)), mode="edge")
    cond_pad = jnp.where(widened > 0.0, widened, edge_pad)
    face_x = harmonic(cond_pad[:, :-1, 1:-1, 1:-1], cond_pad[:, 1:, 1:-1, 1:-1])
    face_y = harmonic(cond_pad[:, 1:-1, :-1, 1:-1], cond_pad[:, 1:-1, 1:, 1:-1])
    face_z = harmonic(cond, cond_pad[:, 1:-1, 1:-1, 2:])
    lower_z = jnp.concatenate([harmonic(cond[..., :1], cond[..., :1]), face_z[..., :-1]], axis=-1)
    return (face_x, face_y, face_z, lower_z)


def operate(values_in, face_x, face_y, face_z, lower_z):
    padded = extend_values(values_in)
    result = face_x[:, 1:] * (values_in - padded[:, 2:, 1:-1, 1:-1]) + face_x[:, :-1] * (
        values_in - padded[:, :-2, 1:-1, 1:-1]
    )
    result = (
        result
        + face_y[:, :, 1:] * (values_in - padded[:, 1:-1, 2:, 1:-1])
        + face_y[:, :, :-1] * (values_in - padded[:, 1:-1, :-2, 1:-1])
    )
    result = (
        result
        + face_z * (values_in - padded[:, 1:-1, 1:-1, 2:])
        + lower_z * (values_in - padded[:, 1:-1, 1:-1, :-2])
    )
    return result


def conjugate(cond, forcing):
    face_x, face_y, face_z, lower_z = face_terms(cond)
    residual = jnp.broadcast_to(forcing[None], cond.shape)
    direction = residual
    solution = jnp.zeros_like(cond)
    norm_now = member_dots(jnp.sum(residual * residual, axis=(1, 2, 3)))
    for iteration in range(ITERS):
        image = operate(direction, face_x, face_y, face_z, lower_z)
        step_size = norm_now / member_dots(jnp.sum(direction * image, axis=(1, 2, 3)))
        solution = solution + step_size[:, None, None, None] * direction
        residual = residual - step_size[:, None, None, None] * image
        if iteration + 1 < ITERS:
            norm_next = member_dots(jnp.sum(residual * residual, axis=(1, 2, 3)))
            direction = residual + (norm_next / norm_now)[:, None, None, None] * direction
            norm_now = norm_next
    return solution


def local(ensemble, source, obs_rows, obs_values, obs_noise, obs_var):
    total_members = ensemble.shape[0]
    block_x, block_y, layers = source.shape
    held_fields = lax.all_to_all(ensemble, "space", split_axis=0, concat_axis=1, tiled=True)
    forcing = lax.all_gather(source, "space", axis=0, tiled=True)
    pressure = conjugate(jnp.exp(held_fields), forcing)
    held_count = pressure.shape[0]
    cells_flat = pressure.reshape(held_count, -1, layers)
    gathered_rows = lax.all_gather(obs_rows, "space", axis=0, tiled=True)
    row_ids = gathered_rows[:, 0]
    peer_ids = jnp.arange(row_ids.shape[0], dtype=jnp.int32)[:, None]
    flat_index = (peer_ids * block_x + row_ids // block_y) * block_y + row_ids % block_y
    picked = jnp.take(cells_flat, flat_index.reshape(-1), axis=1)
    returned = lax.all_to_all(picked, "space", split_axis=1, concat_axis=0, tiled=True)
    predicted = returned.reshape(total_members, 1, 1, -1)
    flat_pred = returned.reshape(total_members, -1)
    inv_sigma = 1.0 / jnp.sqrt(obs_var.reshape(-1))
    spread = (flat_pred - jnp.mean(flat_pred, axis=0)) * inv_sigma
    misfit = (obs_values.reshape(-1) - flat_pred) * inv_sigma + obs_noise.reshape(total_members, -1)
    gram_part = jnp.dot(spread, spread.T, precision=lax.Precision.HIGHEST)
    cross_part = jnp.dot(spread, misfit.T, precision=lax.Precision.HIGHEST)
    gram_sum, cross_sum = lax.psum((gram_part, cross_part), ("member", "space"))
    factor = jnp.linalg.cholesky(
        gram_sum + (total_members - 1.0) * jnp.eye(total_members, dtype=jnp.float32)
    )
    weights = jax.scipy.linalg.cho_solve((factor, True), cross_sum)
    flat_field = ensemble.reshape(total_members, -1)
    anomalies = flat_field - jnp.mean(flat_field, axis=0)
    updated = flat_field + jnp.dot(weights.T, anomalies, precision=lax.Precision.HIGHEST)
    return (updated.reshape(ensemble.shape), predicted)


def solution(mesh):
    in_specs = (
        P(None, "space", "member", None),
        P("space", "member", None),
        P("space", "member", None),
        P("space", "member", None),
        P(None, "space", "member", None),
        P("space", "member", None),
    )
    out_specs = (P(None, "space", "member", None), P(None, "space", "member", None))
    return jax.shard_map(local, mesh=mesh, in_specs=in_specs, out_specs=out_specs, check_vma=False)
```

profile of v0, /device:TPU:0, one launch (start us, length us, event | category | flops | bytes accessed | tf_op | source)
XLA Modules:
  0.0 352.0 jit_solution(3334532213000039188)
XLA Ops:
  7.2 6.4 %all-to-all-start = ((f32[128,2,4,128]{3,2,1,0:T(4,128)}), f32[128,2,4,128]{3,2,1,0:T(4,128)S(1)}, u32[]{:S(2)}, u32[]{:S(2)}) async-start(f32[128,2,4,128]{3,2,1,0:T(4,128)} %param.6), calls=%async_computation | async-start | bytes 1048576 | tf_op jit(solution)/shard_map/all_to_all | solution.py:90
  13.5 21.7 %all_gather.7 = f32[16,4,128]{2,1,0:T(4,128)S(1)} all-gather(f32[2,4,128]{2,1,0:T(4,128)} %param.7), channel_id=1, replica_groups=mesh['member'=4,'space'=8] {'space'}, dimensions={0}, use_global_device_ids=true | all-gather | bytes 36864 | tf_op jit(solution)/shard_map/all_gather | solution.py:91
  35.2 3.4 collective-permute-start.2
  38.7 1.3 collective-permute-start.3
  40.6 1.3 collective-permute-done.2
  41.9 4.8 %collective-permute-done.3 = f32[16,16,1,128]{3,0,2,1:T(8,128)S(1)} collective-permute-done((f32[16,16,1,128]{3,0,2,1:T(8,128)S(1)}, f32[16,16,1,128]{3,0,2,1:T(8,128)S(1)}, u32[]{:S(2)}, u32[]{:S(2)}) %collective-permute-start.3) | collective-permute-done | bytes 131104 | tf_op jit(solution)/shard_map/ppermute | solution.py:17
  47.3 1.7 select_maximum_fusion.6
  49.3 1.2 fusion.81
  50.5 3.7 %collective-permute-start = (f32[16,16,1,128]{3,0,2,1:T(8,128)S(1)}, f32[16,16,1,128]{3,0,2,1:T(8,128)S(1)}, u32[]{:S(2)}, u32[]{:S(2)}) collective-permute-start(f32[16,16,1,128]{3,0,2,1:T(8,128)S(1)} %get-tuple-element.35), channel_id=1, source_target_pairs={{0,8},{8,16},{16,24},{1,9},{9,17},{17,25},{2,10},{10,18},{18,26},{... | collective-permute-start | bytes 393224 | tf_op jit(solution)/shard_map/ppermute | solution.py:16
  54.2 1.3 collective-permute-start.1
  56.0 1.3 copy.25
  57.3 3.7 %collective-permute-done.1 = f32[16,16,1,128]{3,0,2,1:T(8,128)S(1)} collective-permute-done((f32[16,16,1,128]{3,0,2,1:T(8,128)S(1)}, f32[16,16,1,128]{3,0,2,1:T(8,128)S(1)}, u32[]{:S(2)}, u32[]{:S(2)}) %collective-permute-start.1) | collective-permute-done | bytes 131104 | tf_op jit(solution)/shard_map/ppermute | solution.py:17
  61.1 2.7 compare_select_fusion
  67.3 9.0 %all-reduce.7 = (f32[16]{0:T(128)S(1)}, f32[16]{0:T(128)S(1)}) all-reduce(f32[16]{0:T(128)S(1)} %reduce_sum.93, f32[16]{0:T(128)S(1)} %get-tuple-element.20), channel_id=1, replica_groups=mesh['member'=4,'space'=8] {'member'}, use_global_device_ids=true, to_apply=%region_1.2 | all-reduce | flops 32 | bytes 256 | tf_op jit(solution)/shard_map/psum | solution.py:37
  76.6 8.0 %psum.72 = f32[16]{0:T(128)S(1)} all-reduce(f32[16]{0:T(128)S(1)} %multiply_reduce_fusion.4), channel_id=1, replica_groups=mesh['member'=4,'space'=8] {'member'}, use_global_device_ids=true, to_apply=%region_5.6 | all-reduce | flops 16 | bytes 128 | tf_op jit(solution)/shard_map/psum | solution.py:37
  84.8 3.4 collective-permute-start.4
  88.2 1.3 collective-permute-start.5
  89.5 1.2 collective-permute-done.4
  90.7 4.5 %collective-permute-done.5 = f32[16,16,1,128]{3,0,2,1:T(8,128)S(1)} collective-permute-done((f32[16,16,1,128]{3,0,2,1:T(8,128)S(1)}, f32[16,16,1,128]{3,0,2,1:T(8,128)S(1)}, u32[]{:S(2)}, u32[]{:S(2)}) %collective-permute-start.5) | collective-permute-done | bytes 131104 | tf_op jit(solution)/shard_map/ppermute | solution.py:17
  95.6 1.4 multiply_reduce_fusion.3
  97.0 9.8 %psum.73 = f32[16]{0:T(128)S(1)} all-reduce(f32[16]{0:T(128)S(1)} %get-tuple-element.18), channel_id=1, replica_groups=mesh['member'=4,'space'=8] {'member'}, use_global_device_ids=true, to_apply=%region_7.8 | all-reduce | flops 16 | bytes 128 | tf_op jit(solution)/shard_map/psum | solution.py:37
  106.8 1.4 multiply_reduce_fusion.2
  108.2 8.0 %psum.74 = f32[16]{0:T(128)S(1)} all-reduce(f32[16]{0:T(128)S(1)} %get-tuple-element.16), channel_id=1, replica_groups=mesh['member'=4,'space'=8] {'member'}, use_global_device_ids=true, to_apply=%region_9.10 | all-reduce | flops 16 | bytes 128 | tf_op jit(solution)/shard_map/psum | solution.py:37
  117.0 3.5 collective-permute-start.6
  120.6 1.3 collective-permute-start.7
  123.8 8.0 %all-reduce.5 = s32[8]{0:T(128)S(1)} all-reduce(s32[8]{0:T(128)S(1)} %bitcast_dynamic-update-slice_fusion), channel_id=1, replica_groups=mesh['member'=4,'space'=8] {'space'}, use_global_device_ids=true, to_apply=%add.5 | all-reduce | flops 8 | bytes 64 | tf_op jit(solution)/shard_map/squeeze | solution.py:96
  131.8 1.4 select_maximum_fusion.2
  133.2 2.3 multiply_reduce_fusion.1
  135.5 11.6 %psum.75 = f32[16]{0:T(128)S(1)} all-reduce(f32[16]{0:T(128)S(1)} %get-tuple-element.14), channel_id=1, replica_groups=mesh['member'=4,'space'=8] {'member'}, use_global_device_ids=true, to_apply=%region_11.12 | all-reduce | flops 16 | bytes 128 | tf_op jit(solution)/shard_map/psum | solution.py:37
  147.1 1.3 multiply_reduce_fusion
  148.4 7.8 %psum.76 = f32[16]{0:T(128)S(1)} all-reduce(f32[16]{0:T(128)S(1)} %multiply_reduce_fusion), channel_id=1, replica_groups=mesh['member'=4,'space'=8] {'member'}, use_global_device_ids=true, to_apply=%region_13.14 | all-reduce | flops 16 | bytes 128 | tf_op jit(solution)/shard_map/psum | solution.py:37
  156.2 1.4 multiply_add_fusion.1
  157.6 3.7 %collective-permute-start.8 = (f32[16,16,1,128]{3,0,2,1:T(8,128)S(1)}, f32[16,16,1,128]{3,0,2,1:T(8,128)S(1)}, u32[]{:S(2)}, u32[]{:S(2)}) collective-permute-start(f32[16,16,1,128]{3,0,2,1:T(8,128)S(1)} %get-tuple-element.27), channel_id=1, source_target_pairs={{0,8},{8,16},{16,24},{1,9},{9,17},{17,25},{2,10},{10,18},{18,26},{... | collective-permute-start | bytes 393224 | tf_op jit(solution)/shard_map/ppermute | solution.py:16
  161.3 1.3 collective-permute-start.9
  162.7 1.2 collective-permute-done.8
  163.8 4.5 %collective-permute-done.9 = f32[16,16,1,128]{3,0,2,1:T(8,128)S(1)} collective-permute-done((f32[16,16,1,128]{3,0,2,1:T(8,128)S(1)}, f32[16,16,1,128]{3,0,2,1:T(8,128)S(1)}, u32[]{:S(2)}, u32[]{:S(2)}) %collective-permute-start.9) | collective-permute-done | bytes 131104 | tf_op jit(solution)/shard_map/ppermute | solution.py:17
  169.5 1.2 reduce_sum.102
  170.7 8.8 %psum.77 = f32[16]{0:T(128)S(1)} all-reduce(f32[16]{0:T(128)S(1)} %fusion.14), channel_id=1, replica_groups=mesh['member'=4,'space'=8] {'member'}, use_global_device_ids=true, to_apply=%region_15.16 | all-reduce | flops 16 | bytes 128 | tf_op jit(solution)/shard_map/psum | solution.py:37
  181.0 3.4 all-to-all-start.1
  184.7 5.6 %all-to-all-done.1 = f32[16,8,128]{2,0,1:T(8,128)S(1)} async-done(((f32[16,8,128]{2,0,1:T(8,128)}), f32[16,8,128]{2,0,1:T(8,128)S(1)}, u32[]{:S(2)}, u32[]{:S(2)}) %all-to-all-start.1) | async-done | bytes 65568 | tf_op jit(solution)/shard_map/all_to_all | solution.py:100
  190.3 0.9 fusion.88
  191.3 0.9 fusion.89
  192.5 124.4 %all-reduce.10.cloned.1.call-done = (f32[128,128]{1,0:T(8,128)}, f32[128,128]{1,0:T(8,128)}) async-done(((f32[128,128]{1,0:T(8,128)}, f32[128,128]{1,0:T(8,128)}), (f32[128,128]{1,0:T(8,128)}, f32[128,128]{1,0:T(8,128)})) %all-reduce.10.cloned.1.call-update) | async-done | bytes 131088 | tf_op jit(solution)/shard_map/psum | solution.py:108
  317.8 0.9 fusion.73
  318.6 11.7 %cholesky.16 = f32[128,128]{1,0:T(8,128)S(1)} custom-call(f32[128,128]{1,0:T(8,128)S(1)} %fusion.73), custom_call_target="Cholesky" | custom-call | tf_op jit(solution)/shard_map/jit(cholesky)/cholesky | solution.py:109
  331.7 9.8 %custom-call.10 = f32[1,128,128]{1,2,0:T(8,128)S(1)} custom-call(f32[1,128,128]{2,1,0:T(8,128)S(1)} %fusion.67), custom_call_target="InvertDiagBlocksLowerTriangular" | custom-call | tf_op jit(solution)/shard_map/jit(_cho_solve)/triangular_solve | solution.py:112
  341.5 1.1 fusion.71
  343.5 1.0 reshape.365
  (90 shorter events, 15.7 us)
Async XLA Ops:
  7.2 41.8 %all-to-all-start = ((f32[128,2,4,128]{3,2,1,0:T(4,128)}), f32[128,2,4,128]{3,2,1,0:T(4,128)S(1)}, u32[]{:S(2)}, u32[]{:S(2)}) async-start(f32[128,2,4,128]{3,2,1,0:T(4,128)} %param.6), calls=%async_computation | async-start | bytes 1048576 | tf_op jit(solution)/shard_map/all_to_all | solution.py:90
  35.2 6.6 %collective-permute-start.2 = (f32[16,16,1,128]{3,0,2,1:T(8,128)S(1)}, f32[16,16,1,128]{3,0,2,1:T(8,128)S(1)}, u32[]{:S(2)}, u32[]{:S(2)}) collective-permute-start(f32[16,16,1,128]{3,0,2,1:T(8,128)S(1)} %broadcast_in_dim.16), channel_id=1, source_target_pairs={{0,8},{8,16},{16,24},{1,9},{9,17},{17,25},{2,10},{10,18},{18,26},{... | collective-permute-start | bytes 393224 | tf_op jit(solution)/shard_map/ppermute | solution.py:16
  38.7 8.0 %collective-permute-start.3 = (f32[16,16,1,128]{3,0,2,1:T(8,128)S(1)}, f32[16,16,1,128]{3,0,2,1:T(8,128)S(1)}, u32[]{:S(2)}, u32[]{:S(2)}) collective-permute-start(f32[16,16,1,128]{3,0,2,1:T(8,128)S(1)} %broadcast_in_dim.17), channel_id=1, source_target_pairs={{8,0},{16,8},{24,16},{9,1},{17,9},{25,17},{10,2},{18,10},{26,18},{... | collective-permute-start | bytes 393224 | tf_op jit(solution)/shard_map/ppermute | solution.py:17
  46.6 0.6 copy-start.7
  50.5 6.8 %collective-permute-start = (f32[16,16,1,128]{3,0,2,1:T(8,128)S(1)}, f32[16,16,1,128]{3,0,2,1:T(8,128)S(1)}, u32[]{:S(2)}, u32[]{:S(2)}) collective-permute-start(f32[16,16,1,128]{3,0,2,1:T(8,128)S(1)} %get-tuple-element.35), channel_id=1, source_target_pairs={{0,8},{8,16},{16,24},{1,9},{9,17},{17,25},{2,10},{10,18},{18,26},{... | collective-permute-start | bytes 393224 | tf_op jit(solution)/shard_map/ppermute | solution.py:16
  54.2 6.9 %collective-permute-start.1 = (f32[16,16,1,128]{3,0,2,1:T(8,128)S(1)}, f32[16,16,1,128]{3,0,2,1:T(8,128)S(1)}, u32[]{:S(2)}, u32[]{:S(2)}) collective-permute-start(f32[16,16,1,128]{3,0,2,1:T(8,128)S(1)} %get-tuple-element.36), channel_id=1, source_target_pairs={{8,0},{16,8},{24,16},{9,1},{17,9},{25,17},{10,2},{18,10},{26,18},{... | collective-permute-start | bytes 393224 | tf_op jit(solution)/shard_map/ppermute | solution.py:17
  64.2 1.5 copy-start
  64.2 1.6 copy-start.6
  64.2 1.6 copy-start.8
  66.7 28.9 %copy-start.2 = (f32[16,16,4,128]{3,0,2,1:T(8,128)}, f32[16,16,4,128]{3,0,2,1:T(8,128)S(1)}, u32[]{:S(2)}) copy-start(f32[16,16,4,128]{3,0,2,1:T(8,128)S(1)} %get-tuple-element.22) | copy-start | bytes 1572868
  84.8 5.9 %collective-permute-start.4 = (f32[16,16,1,128]{3,0,2,1:T(8,128)S(1)}, f32[16,16,1,128]{3,0,2,1:T(8,128)S(1)}, u32[]{:S(2)}, u32[]{:S(2)}) collective-permute-start(f32[16,16,1,128]{3,0,2,1:T(8,128)S(1)} %get-tuple-element.31), channel_id=1, source_target_pairs={{0,8},{8,16},{16,24},{1,9},{9,17},{17,25},{2,10},{10,18},{18,26},{... | collective-permute-start | bytes 393224 | tf_op jit(solution)/shard_map/ppermute | solution.py:16
  88.2 6.9 %collective-permute-start.5 = (f32[16,16,1,128]{3,0,2,1:T(8,128)S(1)}, f32[16,16,1,128]{3,0,2,1:T(8,128)S(1)}, u32[]{:S(2)}, u32[]{:S(2)}) collective-permute-start(f32[16,16,1,128]{3,0,2,1:T(8,128)S(1)} %get-tuple-element.32), channel_id=1, source_target_pairs={{8,0},{16,8},{24,16},{9,1},{17,9},{25,17},{10,2},{18,10},{26,18},{... | collective-permute-start | bytes 393224 | tf_op jit(solution)/shard_map/ppermute | solution.py:17
  106.8 15.7 %copy-start.12 = (u32[32]{0:T(128)S(1)}, u32[32]{0:T(128)}, u32[]{:S(2)}) copy-start(u32[32]{0:T(128)} %constant.131) | copy-start | bytes 388
  108.2 38.9 %copy-start.1 = (f32[16,16,4,128]{3,0,2,1:T(8,128)}, f32[16,16,4,128]{3,0,2,1:T(8,128)S(1)}, u32[]{:S(2)}) copy-start(f32[16,16,4,128]{3,0,2,1:T(8,128)S(1)} %get-tuple-element.17) | copy-start | bytes 1572868
  117.0 14.7 %collective-permute-start.6 = (f32[16,16,1,128]{3,0,2,1:T(8,128)}, f32[16,16,1,128]{3,0,2,1:T(8,128)S(1)}, u32[]{:S(2)}, u32[]{:S(2)}) collective-permute-start(f32[16,16,1,128]{3,0,2,1:T(8,128)} %get-tuple-element.29), channel_id=1, source_target_pairs={{0,8},{8,16},{16,24},{1,9},{9,17},{17,25},{2,10},{10,18},{18,26},{... | collective-permute-start | bytes 393224 | tf_op jit(solution)/shard_map/ppermute | solution.py:16
  120.6 11.2 %collective-permute-start.7 = (f32[16,16,1,128]{3,0,2,1:T(8,128)}, f32[16,16,1,128]{3,0,2,1:T(8,128)}, u32[]{:S(2)}, u32[]{:S(2)}) collective-permute-start(f32[16,16,1,128]{3,0,2,1:T(8,128)} %get-tuple-element.30), channel_id=1, source_target_pairs={{8,0},{16,8},{24,16},{9,1},{17,9},{25,17},{10,2},{18,10},{26,18},{... | collective-permute-start | bytes 393224 | tf_op jit(solution)/shard_map/ppermute | solution.py:17
  131.7 1.5 copy-start.3
  157.6 11.2 %copy-start.4 = (f32[16,16,4,128]{3,0,2,1:T(8,128)S(1)}, f32[16,16,4,128]{3,0,2,1:T(8,128)}, u32[]{:S(2)}) copy-start(f32[16,16,4,128]{3,0,2,1:T(8,128)} %copy-done.2) | copy-start | bytes 1572868
  157.6 6.2 %collective-permute-start.8 = (f32[16,16,1,128]{3,0,2,1:T(8,128)S(1)}, f32[16,16,1,128]{3,0,2,1:T(8,128)S(1)}, u32[]{:S(2)}, u32[]{:S(2)}) collective-permute-start(f32[16,16,1,128]{3,0,2,1:T(8,128)S(1)} %get-tuple-element.27), channel_id=1, source_target_pairs={{0,8},{8,16},{16,24},{1,9},{9,17},{17,25},{2,10},{10,18},{18,26},{... | collective-permute-start | bytes 393224 | tf_op jit(solution)/shard_map/ppermute | solution.py:16
  161.3 6.9 %collective-permute-start.9 = (f32[16,16,1,128]{3,0,2,1:T(8,128)S(1)}, f32[16,16,1,128]{3,0,2,1:T(8,128)S(1)}, u32[]{:S(2)}, u32[]{:S(2)}) collective-permute-start(f32[16,16,1,128]{3,0,2,1:T(8,128)S(1)} %get-tuple-element.28), channel_id=1, source_target_pairs={{8,0},{16,8},{24,16},{9,1},{17,9},{25,17},{10,2},{18,10},{26,18},{... | collective-permute-start | bytes 393224 | tf_op jit(solution)/shard_map/ppermute | solution.py:17
  169.4 15.2 %copy-start.11 = (f32[1,1,128]{2,1,0:T(1,128)S(1)}, f32[1,1,128]{2,1,0:T(1,128)}, u32[]{:S(2)}) copy-start(f32[1,1,128]{2,1,0:T(1,128)} %param.11) | copy-start | bytes 1540
  169.4 21.8 %copy-start.9 = (f32[128,1,1,128]{3,2,1,0:T(1,128)S(1)}, f32[128,1,1,128]{3,2,1,0:T(1,128)}, u32[]{:S(2)}) copy-start(f32[128,1,1,128]{3,2,1,0:T(1,128)} %param.10) | copy-start | bytes 196612
  169.4 21.8 %copy-start.10 = (f32[1,1,128]{2,1,0:T(1,128)S(1)}, f32[1,1,128]{2,1,0:T(1,128)}, u32[]{:S(2)}) copy-start(f32[1,1,128]{2,1,0:T(1,128)} %param.9) | copy-start | bytes 1540
  170.7 21.5 %copy-start.5 = (f32[128,2,4,128]{3,2,1,0:T(4,128)S(1)}, f32[128,2,4,128]{3,2,1,0:T(4,128)}, u32[]{:S(2)}) copy-start(f32[128,2,4,128]{3,2,1,0:T(4,128)} %param.6) | copy-start | bytes 1572868
  181.0 9.2 %all-to-all-start.1 = ((f32[16,8,128]{2,0,1:T(8,128)}), f32[16,8,128]{2,0,1:T(8,128)S(1)}, u32[]{:S(2)}, u32[]{:S(2)}) async-start(f32[16,8,128]{2,0,1:T(8,128)} %select_bitcast_fusion), calls=%async_computation.1 | async-start | bytes 131072 | tf_op jit(solution)/shard_map/all_to_all | solution.py:100
  184.4 132.4 %all-reduce.10.cloned.1.call-start = ((), (), s32[]{:S(2)}) async-start(), calls=%async_computation.2 | async-start | bytes 262144 | tf_op jit(solution)/shard_map/psum | solution.py:108
Sparse Core Ops, SparseCore 0:
  192.3 124.4 all-reduce.9
where the time goes:
time: 353 us; the launch traced here: 352 us
  waiting for transfers between devices  151 us (43%)
  blocking collectives  92.5 us (26%)
  other arithmetic  45.3 us (13%)
  starting transfers between devices  34.1 us (10%)
  between operations  15.2 us (4%)
  local copies, waits for them, and re-layouts  10.1 us (3%)
  matrix products  3.76 us (1%)
    psum x1, waiting for transfers between devices, local(): gram_sum, cross_sum = lax.psum((gram_part, cross_part), ('member', 'space'))  124 us
    psum x7, blocking collectives, member_dots(): return lax.psum(dot_terms, 'member')  62.9 us
    all_gather x1, blocking collectives, local(): forcing = lax.all_gather(source, 'space', axis=0, tiled=True)  21.7 us
    ppermute x5, starting transfers between devices, padded_2(): before = lax.ppermute(last, axis, up)  17.7 us
    ppermute x5, waiting for transfers between devices, padded_2(): after = lax.ppermute(leading, axis, down)  17.4 us
    another operation x3, other arithmetic, local(): jnp.linalg.cholesky(gram_sum + (total_members - 1.0) * jnp.eye(total_memb...  12.4 us
    another operation x2, other arithmetic, local(): weights = jax.scipy.linalg.cho_solve((factor, True), cross_sum)  10.5 us
    squeeze x1, blocking collectives, local(): row_ids = gathered_rows[:, 0]  7.97 us
  transfers between devices with their start and end apart: 13, of which 9 were waited for; matrix products, arithmetic and copies ran while one was open for 2% of the time, Pallas kernels for 0%

commit v1 on v0

--- a/solution.py
+++ b/solution.py
@@ -1,9 +1,15 @@
+import functools
+
 import jax
 import jax.numpy as jnp
 from jax import lax
+from jax.experimental import pallas as pl
+from jax.experimental.pallas import tpu as pltpu
 from jax.sharding import PartitionSpec as P
 
 ITERS = 4
+AXES = ("member", "space")
+HIGHEST = lax.Precision.HIGHEST
 
 
 def padded_2(x, sides, width):
@@ -23,12 +29,7 @@
     return 2.0 * first_cond * second_cond / (first_cond + second_cond)
 
 
-def extend_cond(cond):
-    widened = padded_2(cond, (("member", 2),), 1)
-    return jnp.pad(widened, ((0, 0), (1, 1), (0, 0), (1, 1)))
-
-
-def extend_values(values_in):
+def extend(values_in):
     widened = padded_2(values_in, (("member", 2),), 1)
     return jnp.pad(widened, ((0, 0), (1, 1), (0, 0), (1, 1)))
 
@@ -38,7 +39,7 @@
 
 
 def face_terms(cond):
-    widened = extend_cond(cond)
+    widened = extend(cond)
     edge_pad = jnp.pad(cond, ((0, 0), (1, 1), (1, 1), (1, 1)), mode="edge")
     cond_pad = jnp.where(widened > 0.0, widened, edge_pad)
     face_x = harmonic(cond_pad[:, :-1, 1:-1, 1:-1], cond_pad[:, 1:, 1:-1, 1:-1])
@@ -49,7 +50,7 @@
 
 
 def operate(values_in, face_x, face_y, face_z, lower_z):
-    padded = extend_values(values_in)
+    padded = extend(values_in)
     result = face_x[:, 1:] * (values_in - padded[:, 2:, 1:-1, 1:-1]) + face_x[:, :-1] * (
         values_in - padded[:, :-2, 1:-1, 1:-1]
     )
@@ -84,7 +85,7 @@
     return solution
 
 
-def local(ensemble, source, obs_rows, obs_values, obs_noise, obs_var):
+def local_split(ensemble, source, obs_rows, obs_values, obs_noise, obs_var):
     total_members = ensemble.shape[0]
     block_x, block_y, layers = source.shape
     held_fields = lax.all_to_all(ensemble, "space", split_axis=0, concat_axis=1, tiled=True)
@@ -103,17 +104,274 @@
     inv_sigma = 1.0 / jnp.sqrt(obs_var.reshape(-1))
     spread = (flat_pred - jnp.mean(flat_pred, axis=0)) * inv_sigma
     misfit = (obs_values.reshape(-1) - flat_pred) * inv_sigma + obs_noise.reshape(total_members, -1)
-    gram_part = jnp.dot(spread, spread.T, precision=lax.Precision.HIGHEST)
-    cross_part = jnp.dot(spread, misfit.T, precision=lax.Precision.HIGHEST)
-    gram_sum, cross_sum = lax.psum((gram_part, cross_part), ("member", "space"))
+    gram_part = jnp.dot(spread, spread.T, precision=HIGHEST)
+    cross_part = jnp.dot(spread, misfit.T, precision=HIGHEST)
+    gram_sum, cross_sum = lax.psum((gram_part, cross_part), AXES)
     factor = jnp.linalg.cholesky(
         gram_sum + (total_members - 1.0) * jnp.eye(total_members, dtype=jnp.float32)
     )
     weights = jax.scipy.linalg.cho_solve((factor, True), cross_sum)
     flat_field = ensemble.reshape(total_members, -1)
     anomalies = flat_field - jnp.mean(flat_field, axis=0)
-    updated = flat_field + jnp.dot(weights.T, anomalies, precision=lax.Precision.HIGHEST)
+    updated = flat_field + jnp.dot(weights.T, anomalies, precision=HIGHEST)
     return (updated.reshape(ensemble.shape), predicted)
+
+
+def vmem_call(kernel, out_shape, scratch, name, *operands):
+    spec = pl.BlockSpec(memory_space=pltpu.VMEM)
+    return pl.pallas_call(
+        kernel,
+        out_shape=jax.ShapeDtypeStruct(out_shape, jnp.float32),
+        in_specs=[spec] * len(operands),
+        out_specs=spec,
+        scratch_shapes=[pltpu.VMEM(s, jnp.float32) for s in scratch],
+        name=name,
+    )(*operands)
+
+
+def total(acc):
+    return jnp.sum(jnp.sum(acc, axis=0, keepdims=True), axis=1, keepdims=True)
+
+
+def pressure_kernel(g_ref, out_ref, e_ref, fx_ref, fy_ref, fz_ref, bd_ref, p_ref, r_ref, q_ref, x_ref, *, dims):
+    n_m, n_s, held, bx, by, n_obs = dims
+    nx, ny = n_s * bx, n_m * by
+    nz = g_ref.shape[1]
+    block = bx * by
+    rows = (held + 1) * block + n_obs
+    lane = lax.broadcasted_iota(jnp.int32, (ny, nz), 1)
+    sub = lax.broadcasted_iota(jnp.int32, (ny, nz), 0)
+
+    def at(j, x):
+        start = (j * nx + x) * ny
+        return pl.ds(start, ny)
+
+    def here(ref, j, x):
+        return ref[at(j, x), :]
+
+    for m in range(n_m):
+        for s in range(n_s):
+            base = (m * n_s + s) * rows
+            for a in range(bx):
+                x = s * bx + a
+                for j in range(held):
+                    e_ref[pl.ds((j * nx + x) * ny + m * by, by), :] = g_ref[
+                        pl.ds(base + j * block + a * by, by), :
+                    ]
+                x_ref[pl.ds(x * ny + m * by, by), :] = g_ref[pl.ds(base + held * block + a * by, by), :]
+
+    edge_z = (lane == 0).astype(jnp.float32) + (lane == nz - 1).astype(jnp.float32)
+    edge_y = (sub == 0).astype(jnp.float32) + (sub == ny - 1).astype(jnp.float32)
+    inner_z = lane > 0
+    inner_y = sub > 0
+    norm0 = jnp.zeros((ny, nz), jnp.float32)
+    for x in range(nx):
+        v = here(x_ref, 0, x)
+        norm0 = norm0 + v * v
+        for j in range(held):
+            p_ref[at(j, x), :] = v
+            r_ref[at(j, x), :] = v
+    norm_now = [total(norm0)] * held
+
+    for j in range(held):
+        before = None
+        for x in range(nx):
+            e = jnp.exp(-here(e_ref, j, x))
+            if before is not None:
+                fx_ref[at(j, x), :] = 2.0 / (e + before)
+            fy_ref[at(j, x), :] = jnp.where(inner_y, 2.0 / (e + pltpu.roll(e, 1, 0)), 0.0)
+            fz_ref[at(j, x), :] = jnp.where(inner_z, 2.0 / (e + pltpu.roll(e, 1, 1)), 0.0)
+            ends = edge_y + edge_z
+            if x == 0 or x == nx - 1:
+                ends = ends + 1.0
+            bd_ref[at(j, x), :] = ends / e
+            before = e
+
+    for iteration in range(ITERS):
+        last = iteration + 1 == ITERS
+        steps = []
+        for j in range(held):
+            acc = jnp.zeros((ny, nz), jnp.float32)
+            v = here(p_ref, j, 0)
+            gx = None
+            for x in range(nx):
+                gy = here(fy_ref, j, x) * (v - pltpu.roll(v, 1, 0))
+                gz = here(fz_ref, j, x) * (v - pltpu.roll(v, 1, 1))
+                image = here(bd_ref, j, x) * v
+                image = image + (gy - pltpu.roll(gy, ny - 1, 0))
+                image = image + (gz - pltpu.roll(gz, nz - 1, 1))
+                if gx is not None:
+                    image = image + gx
+                if x + 1 < nx:
+                    after = here(p_ref, j, x + 1)
+                    gx = here(fx_ref, j, x + 1) * (after - v)
+                    image = image - gx
+                if not last:
+                    q_ref[at(j, x), :] = image
+                acc = acc + v * image
+                if x + 1 < nx:
+                    v = after
+            steps.append(norm_now[j] / total(acc))
+        norm_next = []
+        for j in range(held):
+            step = jnp.broadcast_to(steps[j], (ny, nz))
+            acc = jnp.zeros((ny, nz), jnp.float32)
+            for x in range(nx):
+                add = step * here(p_ref, j, x)
+                x_ref[at(j, x), :] = add if iteration == 0 else here(x_ref, j, x) + add
+                if not last:
+                    res = here(r_ref, j, x) - step * here(q_ref, j, x)
+                    r_ref[at(j, x), :] = res
+                    acc = acc + res * res
+            if not last:
+                norm_next.append(total(acc))
+        if not last:
+            for j in range(held):
+                ratio = jnp.broadcast_to(norm_next[j] / norm_now[j], (ny, nz))
+                for x in range(nx):
+                    p_ref[at(j, x), :] = here(r_ref, j, x) + ratio * here(p_ref, j, x)
+            norm_now = norm_next
+
+    for m in range(n_m):
+        for s in range(n_s):
+            peer = m * n_s + s
+            for o in range(n_obs):
+                picked = g_ref[pl.ds(peer * rows + (held + 1) * block + o, 1), :].astype(jnp.int32)[0, 0]
+                cell = (s * bx + picked // by) * ny + m * by + picked % by
+                for j in range(held):
+                    out_ref[pl.ds((peer * held + j) * n_obs + o, 1), :] = x_ref[pl.ds(j * nx * ny + cell, 1), :]
+
+
+def sums_kernel(pred_ref, values_ref, noise_ref, var_ref, out_ref, *, devices):
+    members = pred_ref.shape[0]
+    held = members // devices
+    pred = pred_ref[...]
+    inv_sigma = 1.0 / jnp.sqrt(var_ref[...])
+    mean = jnp.sum(pred, axis=0, keepdims=True) / members
+    spread = (pred - mean) * inv_sigma
+    misfit = (values_ref[...] - pred) * inv_sigma + noise_ref[...]
+    by_last = (((1,), (1,)), ((), ()))
+    gram = lax.dot_general(spread, spread, by_last, precision=HIGHEST, preferred_element_type=jnp.float32)
+    cross = lax.dot_general(spread, misfit, by_last, precision=HIGHEST, preferred_element_type=jnp.float32)
+    for d in range(devices):
+        out_ref[d, 0:held, :] = gram[d * held : (d + 1) * held, :]
+        out_ref[d, held : 2 * held, :] = cross[d * held : (d + 1) * held, :]
+
+
+def update_kernel(sums_ref, field_ref, out_ref, a_ref, c_ref, *, devices):
+    members = sums_ref.shape[2]
+    held = members // devices
+    tile = 8
+    for d in range(devices):
+        a_ref[pl.ds(d * held, held), :] = sums_ref[d, 0:held, :]
+        c_ref[pl.ds(d * held, held), :] = sums_ref[d, held : 2 * held, :]
+    lane = lax.broadcasted_iota(jnp.int32, (tile, members), 1)
+    sub = lax.broadcasted_iota(jnp.int32, (tile, members), 0)
+    blocks = members // tile
+    left, right = [], []
+    for k in range(blocks):
+        own = (lane == sub + k * tile).astype(jnp.float32) * (members - 1.0)
+        left.append(a_ref[pl.ds(k * tile, tile), :] + own)
+        right.append(c_ref[pl.ds(k * tile, tile), :])
+    wide = (tile, members)
+
+    def row(x, t):
+        return jnp.broadcast_to(x[t : t + 1, :], wide)
+
+    def column(x, t):
+        return jnp.broadcast_to(x[:, t : t + 1], wide)
+
+    for k in range(blocks):
+        parts = [column(left[k], k * tile + t) for t in range(tile)] + [left[k], right[k]]
+        for t in range(tile):
+            inverse = 1.0 / row(parts[t], t)
+            factor = jnp.where(sub == t, 0.0, parts[t] * inverse)
+            scaled = sub == t
+            for i in range(t + 1, len(parts)):
+                pivot = row(parts[i], t)
+                parts[i] = jnp.where(scaled, pivot * inverse, parts[i] - factor * pivot)
+        left[k], right[k] = parts[-2], parts[-1]
+        rows_left = [row(left[k], t) for t in range(tile)]
+        rows_right = [row(right[k], t) for t in range(tile)]
+        for i in range(blocks):
+            if i != k:
+                columns = [column(left[i], k * tile + t) for t in range(tile)]
+                for t in range(tile):
+                    right[i] = right[i] - columns[t] * rows_right[t]
+                    if k + 1 < blocks:
+                        left[i] = left[i] - columns[t] * rows_left[t]
+    for k in range(blocks):
+        c_ref[pl.ds(k * tile, tile), :] = right[k]
+    weights = c_ref[...]
+    cells = field_ref.shape[0] // members
+    by_first = (((0,), (0,)), ((), ()))
+    for c in range(cells):
+        field = field_ref[pl.ds(c, members, stride=cells), :]
+        anomaly = field - jnp.sum(field, axis=0, keepdims=True) / members
+        moved = lax.dot_general(weights, anomaly, by_first, precision=HIGHEST, preferred_element_type=jnp.float32)
+        out_ref[pl.ds(c, members, stride=cells), :] = field + moved
+
+
+def exchange(x):
+    return lax.all_to_all(x, AXES, split_axis=0, concat_axis=0, tiled=True)
+
+
+def local_whole(ensemble, source, obs_rows, obs_values, obs_noise, obs_var):
+    members = ensemble.shape[0]
+    bx, by, nz = source.shape
+    n_m, n_s = lax.axis_size("member"), lax.axis_size("space")
+    devices = n_m * n_s
+    held = members // devices
+    block = bx * by
+    n_obs = obs_rows.shape[-1]
+    wide = (devices, block, 1, nz)
+    packed = jnp.concatenate(
+        [
+            ensemble.reshape(devices, held * block, 1, nz),
+            jnp.broadcast_to(source.reshape(1, block, 1, nz), wide),
+            jnp.broadcast_to(obs_rows.astype(jnp.float32).reshape(1, n_obs, 1, 1), (devices, n_obs, 1, nz)),
+        ],
+        axis=1,
+    )
+    rows = packed.shape[1]
+    got = exchange(packed.reshape(devices * rows, 1, nz)).reshape(devices * rows, nz)
+    nx, ny = n_s * bx, n_m * by
+    field = (held * nx * ny, nz)
+    picked = vmem_call(
+        functools.partial(pressure_kernel, dims=(n_m, n_s, held, bx, by, n_obs)),
+        (members * n_obs, nz),
+        [field] * 9,
+        "pressure",
+        got,
+    )
+    returned = exchange(picked.reshape(members * n_obs, 1, nz))
+    sums = vmem_call(
+        functools.partial(sums_kernel, devices=devices),
+        (devices, 2 * held, members),
+        [],
+        "sums",
+        returned.reshape(members, n_obs * nz),
+        obs_values.reshape(1, -1),
+        obs_noise.reshape(members, -1),
+        obs_var.reshape(1, -1),
+    )
+    own = jnp.sum(exchange(sums), axis=0, keepdims=True)
+    gathered = exchange(jnp.broadcast_to(own, sums.shape))
+    updated = vmem_call(
+        functools.partial(update_kernel, devices=devices),
+        (members * block, nz),
+        [(members, members)] * 2,
+        "update",
+        gathered,
+        ensemble.reshape(members * block, nz),
+    )
+    return (updated.reshape(ensemble.shape), returned.reshape(members, 1, 1, n_obs * nz))
+
+
+def local(ensemble, *rest):
+    devices = lax.axis_size("member") * lax.axis_size("space")
+    form = local_whole if ensemble.shape[0] % devices == 0 else local_split
+    return form(ensemble, *rest)
 
 
 def solution(mesh):

time: 353 us -> 92.6 us (0.26)
  waiting for transfers between devices: 151 us -> 8.16 us
  blocking collectives: 92.5 us -> 48 us
  other arithmetic: 45.3 us -> 1.7 us
  starting transfers between devices: 34.1 us -> 2.58 us
  Pallas kernels: 0 us -> 27.7 us
  between operations: 15.2 us -> 1.31 us
  local copies, waits for them, and re-layouts: 10.1 us -> 2.69 us
  matrix products: 3.76 us -> 0 us
    psum x1 -> x0, waiting for transfers between devices: 124 us -> none  [local(): gram_sum, cross_sum = lax.psum((gram_part, cross_part), ('member', 'space'))]
    psum x7 -> x0, blocking collectives: 62.9 us -> none  [member_dots(): return lax.psum(dot_terms, 'member')]
    all_to_all x0 -> x3, blocking collectives: none -> 48 us  [exchange(): return lax.all_to_all(x, AXES, split_axis=0, concat_axis=0, tiled=True)]
    pallas_call x0 -> x3, Pallas kernels: none -> 27.7 us  [vmem_call(): pl.pallas_call(kernel, out_shape=jax.ShapeDtypeStruct(out_shape, jnp.floa...]
    ppermute x10 -> x0, starting transfers between devices: 24.2 us -> none  [the longest x5 17.7 us: padded_2(): before = lax.ppermute(last, axis, up)]
    another operation x5 -> x0, other arithmetic: 22.9 us -> none  [the longest x3 12.4 us: local(): jnp.linalg.cholesky(gram_sum + (total_members - 1.0) * jnp.eye(total_memb...]
    all_gather x1 -> x0, blocking collectives: 21.7 us -> none  [local(): forcing = lax.all_gather(source, 'space', axis=0, tiled=True)]
    ppermute x10 -> x0, waiting for transfers between devices: 21.1 us -> none  [the longest x5 17.4 us: padded_2(): after = lax.ppermute(leading, axis, down)]
  transfers between devices with their start and end apart: 13 -> 1, of which waited for: 9 -> 1; matrix products, arithmetic and copies ran while one was open for 2% -> 0% of each run, Pallas kernels for 0% -> 0%
where the time goes in v1:
time: 92.6 us; the launch traced here: 92.1 us
  blocking collectives  48 us (52%)
  Pallas kernels  27.7 us (30%)
  waiting for transfers between devices  8.16 us (9%)
  local copies, waits for them, and re-layouts  2.69 us (3%)
  starting transfers between devices  2.58 us (3%)
  other arithmetic  1.7 us (2%)
  between operations  1.31 us (1%)
    all_to_all x3, blocking collectives, exchange(): return lax.all_to_all(x, AXES, split_axis=0, concat_axis=0, tiled=True)  48 us
    pallas_call x3, Pallas kernels, vmem_call(): pl.pallas_call(kernel, out_shape=jax.ShapeDtypeStruct(out_shape, jnp.floa...  27.7 us
    all_to_all x1, waiting for transfers between devices, exchange(): return lax.all_to_all(x, AXES, split_axis=0, concat_axis=0, tiled=True)  8.16 us
    all_to_all x1, starting transfers between devices, exchange(): return lax.all_to_all(x, AXES, split_axis=0, concat_axis=0, tiled=True)  2.58 us
    unnamed x7, local copies, waits for them, and re-layouts  1.88 us
  transfers between devices with their start and end apart: 1, of which 1 were waited for; matrix products, arithmetic and copies ran while one was open for 0% of the time, Pallas kernels for 0%

profile of v1, /device:TPU:0, one launch (start us, length us, event | category | flops | bytes accessed | tf_op | source)
XLA Modules:
  0.0 92.1 jit_solution(3379878607558588779)
XLA Ops:
  1.3 0.0 copy-start.2
  1.3 0.1 pad.2.clone
  1.4 0.6 copy-done.2
  2.0 0.1 broadcast_in_dim.21
  2.0 1.7 %maximum_maximum_fusion = f32[32,41,1,128]{3,2,1,0:T(1,128)S(1)} fusion(f32[32,8,1,128]{3,2,1,0:T(1,128)S(1)} %broadcast_in_dim.21, f32[32,32,1,128]{3,2,1,0:T(1,128)} %bitcast.23, f32[41]{0:T(128)S(1)} %pad.2.clone), kind=kLoop, calls=%fused_computation | loop fusion | flops 335872 | bytes 1327268 | tf_op jit(solution)/shard_map/concatenate | solution.py:328
  3.7 26.6 %all_to_all.20 = f32[1312,1,128]{2,1,0:T(1,128)} all-to-all(f32[1312,1,128]{2,1,0:T(1,128)S(1)} %bitcast.21), channel_id=1, replica_groups=mesh['member'=4,'space'=8] {'member','space'}, dimensions={0} | all-to-all | bytes 1343488 | tf_op jit(solution)/shard_map/all_to_all | solution.py:316
  30.3 19.0 %pressure.1 = f32[128,128]{1,0:T(8,128)} custom-call(f32[1312,128]{1,0:T(8,128)} %bitcast.22), custom_call_target="tpu_custom_call" | custom-call | tf_op jit(solution)/shard_map/pressure/pallas_call | solution.py:122
  49.4 10.6 %all_to_all.21 = f32[128,1,128]{2,1,0:T(1,128)} all-to-all(f32[128,1,128]{2,1,0:T(1,128)} %bitcast.28), channel_id=1, replica_groups=mesh['member'=4,'space'=8] {'member','space'}, dimensions={0} | all-to-all | bytes 131072 | tf_op jit(solution)/shard_map/all_to_all | solution.py:316
  60.0 1.9 %sums.1 = f32[32,8,128]{2,1,0:T(8,128)} custom-call(f32[128,128]{1,0:T(8,128)} %bitcast.25, f32[1,128]{1,0:T(1,128)} %bitcast.31, f32[128,128]{1,0:T(8,128)} %bitcast.29, f32[1,128]{1,0:T(1,128)} %bitcast.32), custom_call_target="tpu_custom_call" | custom-call | tf_op jit(solution)/shard_map/sums/pallas_call | solution.py:122
  61.9 10.7 %all_to_all.22 = f32[32,8,128]{2,1,0:T(8,128)S(1)} all-to-all(f32[32,8,128]{2,1,0:T(8,128)} %sums.1), channel_id=1, replica_groups=mesh['member'=4,'space'=8] {'member','space'}, dimensions={0} | all-to-all | bytes 262144 | tf_op jit(solution)/shard_map/all_to_all | solution.py:316
  72.7 0.7 broadcast_in_dim.24
  73.4 2.6 %all-to-all-start.3 = ((f32[32,8,128]{2,1,0:T(8,128)}), f32[32,8,128]{2,1,0:T(8,128)S(1)}, u32[]{:S(2)}, u32[]{:S(2)}) async-start(f32[32,8,128]{2,1,0:T(8,128)} %broadcast_in_dim.24), calls=%async_computation.3 | async-start | bytes 262144 | tf_op jit(solution)/shard_map/all_to_all | solution.py:316
  76.0 8.2 %all-to-all-done.3.sums_ref = f32[32,8,128]{2,1,0:T(8,128)S(1)} async-done(((f32[32,8,128]{2,1,0:T(8,128)}), f32[32,8,128]{2,1,0:T(8,128)S(1)}, u32[]{:S(2)}, u32[]{:S(2)}) %all-to-all-start.3) | async-done | bytes 131104 | tf_op jit(solution)/shard_map/all_to_all | solution.py:316
  84.1 0.0 copy-start.1
  84.1 0.6 copy-done.1
  84.8 0.0 copy-start
  84.8 6.7 %update.1 = f32[1024,128]{1,0:T(8,128)} custom-call(f32[32,8,128]{2,1,0:T(8,128)} %copy-done.1, f32[1024,128]{1,0:T(8,128)} %bitcast.24), custom_call_target="tpu_custom_call" | custom-call | tf_op jit(solution)/shard_map/update/pallas_call | solution.py:122
  91.5 0.0 copy-done
  91.5 0.6 copy.17
  (1 shorter events, 0.0 us)
Async XLA Ops:
  1.3 0.7 copy-start.2
  73.4 10.7 %all-to-all-start.3 = ((f32[32,8,128]{2,1,0:T(8,128)}), f32[32,8,128]{2,1,0:T(8,128)S(1)}, u32[]{:S(2)}, u32[]{:S(2)}) async-start(f32[32,8,128]{2,1,0:T(8,128)} %broadcast_in_dim.24), calls=%async_computation.3 | async-start | bytes 262144 | tf_op jit(solution)/shard_map/all_to_all | solution.py:316
  84.1 0.6 copy-start.1
  84.8 6.7 %copy-start = (f32[128,1,128]{2,1,0:T(1,128)S(1)}, f32[128,1,128]{2,1,0:T(1,128)}, u32[]{:S(2)}) copy-start(f32[128,1,128]{2,1,0:T(1,128)} %all_to_all.21) | copy-start | bytes 196612

commit v2 on v1

--- a/solution.py
+++ b/solution.py
@@ -133,21 +133,28 @@
     return jnp.sum(jnp.sum(acc, axis=0, keepdims=True), axis=1, keepdims=True)
 
 
-def pressure_kernel(g_ref, out_ref, e_ref, fx_ref, fy_ref, fz_ref, bd_ref, p_ref, r_ref, q_ref, x_ref, *, dims):
+def pressure_kernel(g_ref, out_ref, e_ref, fx_ref, fy_ref, fz_ref, bd_ref, p_ref, r_ref, q_ref, x_ref, acc_ref, norm_ref, *, dims):
     n_m, n_s, held, bx, by, n_obs = dims
     nx, ny = n_s * bx, n_m * by
     nz = g_ref.shape[1]
     block = bx * by
     rows = (held + 1) * block + n_obs
-    lane = lax.broadcasted_iota(jnp.int32, (ny, nz), 1)
-    sub = lax.broadcasted_iota(jnp.int32, (ny, nz), 0)
+    plane = (ny, nz)
+    lane = lax.broadcasted_iota(jnp.int32, plane, 1)
+    sub = lax.broadcasted_iota(jnp.int32, plane, 0)
 
     def at(j, x):
-        start = (j * nx + x) * ny
-        return pl.ds(start, ny)
-
-    def here(ref, j, x):
-        return ref[at(j, x), :]
+        return pl.ds(pl.multiple_of((j * nx + x) * ny, ny), ny)
+
+    def member(j):
+        return pl.ds(pl.multiple_of(j * ny, ny), ny)
+
+    def for_members(fn):
+        def body(j, carry):
+            fn(j)
+            return carry
+
+        lax.fori_loop(0, held, body, 0)
 
     for m in range(n_m):
         for s in range(n_s):
@@ -162,75 +169,101 @@
 
     edge_z = (lane == 0).astype(jnp.float32) + (lane == nz - 1).astype(jnp.float32)
     edge_y = (sub == 0).astype(jnp.float32) + (sub == ny - 1).astype(jnp.float32)
-    inner_z = lane > 0
-    inner_y = sub > 0
-    norm0 = jnp.zeros((ny, nz), jnp.float32)
+    norm0 = jnp.zeros(plane, jnp.float32)
     for x in range(nx):
-        v = here(x_ref, 0, x)
+        v = x_ref[at(0, x), :]
         norm0 = norm0 + v * v
         for j in range(held):
             p_ref[at(j, x), :] = v
             r_ref[at(j, x), :] = v
-    norm_now = [total(norm0)] * held
-
+    norm0 = jnp.broadcast_to(total(norm0), plane)
     for j in range(held):
+        norm_ref[member(j), :] = norm0
+
+    def faces(j):
         before = None
         for x in range(nx):
-            e = jnp.exp(-here(e_ref, j, x))
+            e = jnp.exp(-e_ref[at(j, x), :])
             if before is not None:
                 fx_ref[at(j, x), :] = 2.0 / (e + before)
-            fy_ref[at(j, x), :] = jnp.where(inner_y, 2.0 / (e + pltpu.roll(e, 1, 0)), 0.0)
-            fz_ref[at(j, x), :] = jnp.where(inner_z, 2.0 / (e + pltpu.roll(e, 1, 1)), 0.0)
+            fy_ref[at(j, x), :] = jnp.where(sub > 0, 2.0 / (e + pltpu.roll(e, 1, 0)), 0.0)
+            fz_ref[at(j, x), :] = jnp.where(lane > 0, 2.0 / (e + pltpu.roll(e, 1, 1)), 0.0)
             ends = edge_y + edge_z
             if x == 0 or x == nx - 1:
                 ends = ends + 1.0
             bd_ref[at(j, x), :] = ends / e
             before = e
 
-    for iteration in range(ITERS):
-        last = iteration + 1 == ITERS
-        steps = []
-        for j in range(held):
-            acc = jnp.zeros((ny, nz), jnp.float32)
-            v = here(p_ref, j, 0)
-            gx = None
-            for x in range(nx):
-                gy = here(fy_ref, j, x) * (v - pltpu.roll(v, 1, 0))
-                gz = here(fz_ref, j, x) * (v - pltpu.roll(v, 1, 1))
-                image = here(bd_ref, j, x) * v
-                image = image + (gy - pltpu.roll(gy, ny - 1, 0))
-                image = image + (gz - pltpu.roll(gz, nz - 1, 1))
-                if gx is not None:
-                    image = image + gx
-                if x + 1 < nx:
-                    after = here(p_ref, j, x + 1)
-                    gx = here(fx_ref, j, x + 1) * (after - v)
-                    image = image - gx
-                if not last:
-                    q_ref[at(j, x), :] = image
-                acc = acc + v * image
-                if x + 1 < nx:
-                    v = after
-            steps.append(norm_now[j] / total(acc))
-        norm_next = []
-        for j in range(held):
-            step = jnp.broadcast_to(steps[j], (ny, nz))
-            acc = jnp.zeros((ny, nz), jnp.float32)
-            for x in range(nx):
-                add = step * here(p_ref, j, x)
-                x_ref[at(j, x), :] = add if iteration == 0 else here(x_ref, j, x) + add
-                if not last:
-                    res = here(r_ref, j, x) - step * here(q_ref, j, x)
-                    r_ref[at(j, x), :] = res
-                    acc = acc + res * res
-            if not last:
-                norm_next.append(total(acc))
-        if not last:
-            for j in range(held):
-                ratio = jnp.broadcast_to(norm_next[j] / norm_now[j], (ny, nz))
-                for x in range(nx):
-                    p_ref[at(j, x), :] = here(r_ref, j, x) + ratio * here(p_ref, j, x)
-            norm_now = norm_next
+    for_members(faces)
+
+    def along_z(j):
+        for x in range(nx):
+            v = p_ref[at(j, x), :]
+            gz = fz_ref[at(j, x), :] * (v - pltpu.roll(v, 1, 1))
+            q_ref[at(j, x), :] = gz - pltpu.roll(gz, nz - 1, 1)
+
+    def apply(j):
+        acc = jnp.zeros(plane, jnp.float32)
+        v = p_ref[at(j, 0), :]
+        gx = None
+        for x in range(nx):
+            gy = fy_ref[at(j, x), :] * (v - pltpu.roll(v, 1, 0))
+            image = q_ref[at(j, x), :] + bd_ref[at(j, x), :] * v
+            image = image + (gy - pltpu.roll(gy, ny - 1, 0))
+            if gx is not None:
+                image = image + gx
+            if x + 1 < nx:
+                after = p_ref[at(j, x + 1), :]
+                gx = fx_ref[at(j, x + 1), :] * (after - v)
+                image = image - gx
+            q_ref[at(j, x), :] = image
+            acc = acc + v * image
+            if x + 1 < nx:
+                v = after
+        acc_ref[member(j), :] = acc
+
+    def totals():
+        return [jnp.broadcast_to(total(acc_ref[member(j), :]), plane) for j in range(held)]
+
+    def multiply():
+        for_members(along_z)
+        for_members(apply)
+        for j, dot in enumerate(totals()):
+            acc_ref[member(j), :] = norm_ref[member(j), :] / dot
+
+    def move(j):
+        step = acc_ref[member(j), :]
+        for x in range(nx):
+            x_ref[at(j, x), :] = x_ref[at(j, x), :] + step * p_ref[at(j, x), :]
+
+    def move_and_leave(j):
+        step = acc_ref[member(j), :]
+        acc = jnp.zeros(plane, jnp.float32)
+        for x in range(nx):
+            x_ref[at(j, x), :] = x_ref[at(j, x), :] + step * p_ref[at(j, x), :]
+            res = r_ref[at(j, x), :] - step * q_ref[at(j, x), :]
+            r_ref[at(j, x), :] = res
+            acc = acc + res * res
+        acc_ref[member(j), :] = acc
+
+    def turn(j):
+        ratio = acc_ref[member(j), :]
+        for x in range(nx):
+            p_ref[at(j, x), :] = r_ref[at(j, x), :] + ratio * p_ref[at(j, x), :]
+
+    def one(iteration, carry):
+        multiply()
+        for_members(move_and_leave)
+        for j, norm in enumerate(totals()):
+            acc_ref[member(j), :] = norm / norm_ref[member(j), :]
+            norm_ref[member(j), :] = norm
+        for_members(turn)
+        return carry
+
+    x_ref[...] = jnp.zeros(x_ref.shape, jnp.float32)
+    lax.fori_loop(0, ITERS - 1, one, 0)
+    multiply()
+    for_members(move)
 
     for m in range(n_m):
         for s in range(n_s):
@@ -340,7 +373,7 @@
     picked = vmem_call(
         functools.partial(pressure_kernel, dims=(n_m, n_s, held, bx, by, n_obs)),
         (members * n_obs, nz),
-        [field] * 9,
+        [field] * 9 + [(held * ny, nz)] * 2,
         "pressure",
         got,
     )

time: 92.6 us -> 81.6 us (0.88)
  Pallas kernels: 27.7 us -> 16.7 us
    pallas_call x3, Pallas kernels: 27.7 us -> 16.7 us  [vmem_call(): pl.pallas_call(kernel, out_shape=jax.ShapeDtypeStruct(out_shape, jnp.floa...]
where the time goes in v2:
time: 81.6 us; the launch traced here: 81.1 us
  blocking collectives  48 us (59%)
  Pallas kernels  16.7 us (20%)
  waiting for transfers between devices  8.16 us (10%)
  local copies, waits for them, and re-layouts  2.69 us (3%)
  starting transfers between devices  2.58 us (3%)
  other arithmetic  1.7 us (2%)
  between operations  1.31 us (2%)
    all_to_all x3, blocking collectives, exchange(): return lax.all_to_all(x, AXES, split_axis=0, concat_axis=0, tiled=True)  48 us
    pallas_call x3, Pallas kernels, vmem_call(): pl.pallas_call(kernel, out_shape=jax.ShapeDtypeStruct(out_shape, jnp.floa...  16.7 us
    all_to_all x1, waiting for transfers between devices, exchange(): return lax.all_to_all(x, AXES, split_axis=0, concat_axis=0, tiled=True)  8.16 us
    all_to_all x1, starting transfers between devices, exchange(): return lax.all_to_all(x, AXES, split_axis=0, concat_axis=0, tiled=True)  2.58 us
    unnamed x7, local copies, waits for them, and re-layouts  1.88 us
    concatenate x1, other arithmetic, local_whole(): jnp.concatenate([ensemble.reshape(devices, held * block, 1, nz), jnp.broa...  1.67 us
  transfers between devices with their start and end apart: 1, of which 1 were waited for; matrix products, arithmetic and copies ran while one was open for 0% of the time, Pallas kernels for 0%

profile of v2, /device:TPU:0, one launch (start us, length us, event | category | flops | bytes accessed | tf_op | source)
XLA Modules:
  0.0 81.1 jit_solution(10619022438274838945)
XLA Ops:
  1.3 0.0 copy-start.2
  1.3 0.1 pad.2.clone
  1.4 0.6 copy-done.2
  2.0 0.1 broadcast_in_dim.21
  2.0 1.7 %maximum_maximum_fusion = f32[32,41,1,128]{3,2,1,0:T(1,128)S(1)} fusion(f32[32,8,1,128]{3,2,1,0:T(1,128)S(1)} %broadcast_in_dim.21, f32[32,32,1,128]{3,2,1,0:T(1,128)} %bitcast.23, f32[41]{0:T(128)S(1)} %pad.2.clone), kind=kLoop, calls=%fused_computation | loop fusion | flops 335872 | bytes 1327268 | tf_op jit(solution)/shard_map/concatenate | solution.py:361
  3.7 26.6 %all_to_all.20 = f32[1312,1,128]{2,1,0:T(1,128)} all-to-all(f32[1312,1,128]{2,1,0:T(1,128)S(1)} %bitcast.21), channel_id=1, replica_groups=mesh['member'=4,'space'=8] {'member','space'}, dimensions={0} | all-to-all | bytes 1343488 | tf_op jit(solution)/shard_map/all_to_all | solution.py:349
  30.3 8.0 %pressure.1 = f32[128,128]{1,0:T(8,128)} custom-call(f32[1312,128]{1,0:T(8,128)} %bitcast.22), custom_call_target="tpu_custom_call" | custom-call | tf_op jit(solution)/shard_map/pressure/pallas_call | solution.py:122
  38.4 10.6 %all_to_all.21 = f32[128,1,128]{2,1,0:T(1,128)} all-to-all(f32[128,1,128]{2,1,0:T(1,128)} %bitcast.28), channel_id=1, replica_groups=mesh['member'=4,'space'=8] {'member','space'}, dimensions={0} | all-to-all | bytes 131072 | tf_op jit(solution)/shard_map/all_to_all | solution.py:349
  49.0 1.9 %sums.1 = f32[32,8,128]{2,1,0:T(8,128)} custom-call(f32[128,128]{1,0:T(8,128)} %bitcast.25, f32[1,128]{1,0:T(1,128)} %bitcast.31, f32[128,128]{1,0:T(8,128)} %bitcast.29, f32[1,128]{1,0:T(1,128)} %bitcast.32), custom_call_target="tpu_custom_call" | custom-call | tf_op jit(solution)/shard_map/sums/pallas_call | solution.py:122
  50.9 10.7 %all_to_all.22 = f32[32,8,128]{2,1,0:T(8,128)S(1)} all-to-all(f32[32,8,128]{2,1,0:T(8,128)} %sums.1), channel_id=1, replica_groups=mesh['member'=4,'space'=8] {'member','space'}, dimensions={0} | all-to-all | bytes 262144 | tf_op jit(solution)/shard_map/all_to_all | solution.py:349
  61.7 0.7 broadcast_in_dim.24
  62.4 2.6 %all-to-all-start.3 = ((f32[32,8,128]{2,1,0:T(8,128)}), f32[32,8,128]{2,1,0:T(8,128)S(1)}, u32[]{:S(2)}, u32[]{:S(2)}) async-start(f32[32,8,128]{2,1,0:T(8,128)} %broadcast_in_dim.24), calls=%async_computation.3 | async-start | bytes 262144 | tf_op jit(solution)/shard_map/all_to_all | solution.py:349
  65.0 8.2 %all-to-all-done.3.sums_ref = f32[32,8,128]{2,1,0:T(8,128)S(1)} async-done(((f32[32,8,128]{2,1,0:T(8,128)}), f32[32,8,128]{2,1,0:T(8,128)S(1)}, u32[]{:S(2)}, u32[]{:S(2)}) %all-to-all-start.3) | async-done | bytes 131104 | tf_op jit(solution)/shard_map/all_to_all | solution.py:349
  73.1 0.0 copy-start.1
  73.1 0.6 copy-done.1
  73.8 0.0 copy-start
  73.8 6.7 %update.1 = f32[1024,128]{1,0:T(8,128)} custom-call(f32[32,8,128]{2,1,0:T(8,128)} %copy-done.1, f32[1024,128]{1,0:T(8,128)} %bitcast.24), custom_call_target="tpu_custom_call" | custom-call | tf_op jit(solution)/shard_map/update/pallas_call | solution.py:122
  80.5 0.0 copy-done
  80.5 0.6 copy.17
  (1 shorter events, 0.0 us)
Async XLA Ops:
  1.3 0.7 copy-start.2
  62.4 10.7 %all-to-all-start.3 = ((f32[32,8,128]{2,1,0:T(8,128)}), f32[32,8,128]{2,1,0:T(8,128)S(1)}, u32[]{:S(2)}, u32[]{:S(2)}) async-start(f32[32,8,128]{2,1,0:T(8,128)} %broadcast_in_dim.24), calls=%async_computation.3 | async-start | bytes 262144 | tf_op jit(solution)/shard_map/all_to_all | solution.py:349
  73.1 0.6 copy-start.1
  73.8 6.7 %copy-start = (f32[128,1,128]{2,1,0:T(1,128)S(1)}, f32[128,1,128]{2,1,0:T(1,128)}, u32[]{:S(2)}) copy-start(f32[128,1,128]{2,1,0:T(1,128)} %all_to_all.21) | copy-start | bytes 196612

commit v3 on v2

--- a/solution.py
+++ b/solution.py
@@ -117,16 +117,38 @@
     return (updated.reshape(ensemble.shape), predicted)
 
 
-def vmem_call(kernel, out_shape, scratch, name, *operands):
-    spec = pl.BlockSpec(memory_space=pltpu.VMEM)
+def vmem_call(kernel, out, scratch, name, *operands, spaces=None):
+    specs = [pl.BlockSpec(memory_space=s) for s in spaces or [pltpu.VMEM] * len(operands)]
     return pl.pallas_call(
         kernel,
-        out_shape=jax.ShapeDtypeStruct(out_shape, jnp.float32),
-        in_specs=[spec] * len(operands),
-        out_specs=spec,
-        scratch_shapes=[pltpu.VMEM(s, jnp.float32) for s in scratch],
+        out_shape=out,
+        in_specs=specs,
+        out_specs=pl.BlockSpec(memory_space=pltpu.VMEM),
+        scratch_shapes=scratch,
         name=name,
     )(*operands)
+
+
+def near(x):
+    return pltpu.with_memory_space_constraint(x, pltpu.VMEM)
+
+
+def pack_kernel(field_ref, source_ref, obs_ref, out_ref, sems):
+    devices, rows, _, nz = out_ref.shape
+    cells, block, n_obs = field_ref.shape[1], source_ref.shape[0], obs_ref.shape[0]
+    copies = [
+        pltpu.make_async_copy(field_ref.at[d], out_ref.at[d, pl.ds(0, cells)], sems.at[d]) for d in range(devices)
+    ]
+    for copy in copies:
+        copy.start()
+    source = source_ref[...]
+    picks = [jnp.full((1, 1, nz), obs_ref[o].astype(jnp.float32)) for o in range(n_obs)]
+    for d in range(devices):
+        out_ref[d, pl.ds(cells, block)] = source
+        for o in range(n_obs):
+            out_ref[d, pl.ds(cells + block + o, 1)] = picks[o]
+    for copy in copies:
+        copy.wait()
 
 
 def total(acc):
@@ -357,46 +379,48 @@
     held = members // devices
     block = bx * by
     n_obs = obs_rows.shape[-1]
-    wide = (devices, block, 1, nz)
-    packed = jnp.concatenate(
-        [
-            ensemble.reshape(devices, held * block, 1, nz),
-            jnp.broadcast_to(source.reshape(1, block, 1, nz), wide),
-            jnp.broadcast_to(obs_rows.astype(jnp.float32).reshape(1, n_obs, 1, 1), (devices, n_obs, 1, nz)),
-        ],
-        axis=1,
-    )
-    rows = packed.shape[1]
+    rows = (held + 1) * block + n_obs
+    packed = vmem_call(
+        pack_kernel,
+        pltpu.VMEM((devices, rows, 1, nz), jnp.float32),
+        [pltpu.SemaphoreType.DMA((devices,))],
+        "pack",
+        ensemble.reshape(devices, held * block, 1, nz),
+        source.reshape(block, 1, nz),
+        obs_rows.reshape(-1),
+        spaces=[pl.ANY, pltpu.VMEM, pltpu.SMEM],
+    )
     got = exchange(packed.reshape(devices * rows, 1, nz)).reshape(devices * rows, nz)
     nx, ny = n_s * bx, n_m * by
-    field = (held * nx * ny, nz)
+    field = pltpu.VMEM((held * nx * ny, nz), jnp.float32)
+    plane = pltpu.VMEM((held * ny, nz), jnp.float32)
     picked = vmem_call(
         functools.partial(pressure_kernel, dims=(n_m, n_s, held, bx, by, n_obs)),
-        (members * n_obs, nz),
-        [field] * 9 + [(held * ny, nz)] * 2,
+        pltpu.VMEM((members * n_obs, nz), jnp.float32),
+        [field] * 9 + [plane] * 2,
         "pressure",
-        got,
+        near(got),
     )
     returned = exchange(picked.reshape(members * n_obs, 1, nz))
     sums = vmem_call(
         functools.partial(sums_kernel, devices=devices),
-        (devices, 2 * held, members),
+        pltpu.VMEM((devices, 2 * held, members), jnp.float32),
         [],
         "sums",
-        returned.reshape(members, n_obs * nz),
+        near(returned.reshape(members, n_obs * nz)),
         obs_values.reshape(1, -1),
-        obs_noise.reshape(members, -1),
+        near(obs_noise.reshape(members, -1)),
         obs_var.reshape(1, -1),
     )
     own = jnp.sum(exchange(sums), axis=0, keepdims=True)
     gathered = exchange(jnp.broadcast_to(own, sums.shape))
     updated = vmem_call(
         functools.partial(update_kernel, devices=devices),
-        (members * block, nz),
-        [(members, members)] * 2,
+        jax.ShapeDtypeStruct((members * block, nz), jnp.float32),
+        [pltpu.VMEM((members, members), jnp.float32)] * 2,
         "update",
-        gathered,
-        ensemble.reshape(members * block, nz),
+        near(gathered),
+        near(ensemble.reshape(members * block, nz)),
     )
     return (updated.reshape(ensemble.shape), returned.reshape(members, 1, 1, n_obs * nz))
 

time: 81.6 us -> 74.7 us (0.915)
  blocking collectives: 48 us -> 45.9 us
  Pallas kernels: 16.7 us -> 14.9 us
  other arithmetic: 1.7 us -> 0.04 us
  local copies, waits for them, and re-layouts: 2.69 us -> 1.31 us
    all_to_all x3, blocking collectives: 48 us -> 45.9 us  [exchange(): return lax.all_to_all(x, AXES, split_axis=0, concat_axis=0, tiled=True)]
    pallas_call x3 -> x4, Pallas kernels: 16.7 us -> 14.9 us  [vmem_call(): pl.pallas_call(kernel, out_shape=out, in_specs=specs, out_specs=pl.BlockS...]
    concatenate x1 -> x0, other arithmetic: 1.67 us -> none  [local_whole(): jnp.concatenate([ensemble.reshape(devices, held * block, 1, nz), jnp.broa...]
    unnamed x7 -> x5, local copies, waits for them, and re-layouts: 1.88 us -> 0.64 us
where the time goes in v3:
time: 74.7 us; the launch traced here: 74.2 us
  blocking collectives  45.9 us (61%)
  Pallas kernels  14.9 us (20%)
  waiting for transfers between devices  8.16 us (11%)
  starting transfers between devices  2.58 us (3%)
  between operations  1.32 us (2%)
  local copies, waits for them, and re-layouts  1.31 us (2%)
    all_to_all x3, blocking collectives, exchange(): return lax.all_to_all(x, AXES, split_axis=0, concat_axis=0, tiled=True)  45.9 us
    pallas_call x4, Pallas kernels, vmem_call(): pl.pallas_call(kernel, out_shape=out, in_specs=specs, out_specs=pl.BlockS...  14.9 us
    all_to_all x1, waiting for transfers between devices, exchange(): return lax.all_to_all(x, AXES, split_axis=0, concat_axis=0, tiled=True)  8.16 us
    all_to_all x1, starting transfers between devices, exchange(): return lax.all_to_all(x, AXES, split_axis=0, concat_axis=0, tiled=True)  2.58 us
  transfers between devices with their start and end apart: 1, of which 1 were waited for; matrix products, arithmetic and copies ran while one was open for 0% of the time, Pallas kernels for 0%

profile of v3, /device:TPU:0, one launch (start us, length us, event | category | flops | bytes accessed | tf_op | source)
XLA Modules:
  0.0 74.2 jit_solution(37218480169399629)
XLA Ops:
  1.3 2.0 %pack.1 = f32[32,41,1,128]{3,2,1,0:T(1,128)S(1)} custom-call(f32[32,32,1,128]{3,2,1,0:T(1,128)} %bitcast.22, f32[8,1,128]{2,1,0:T(1,128)} %bitcast.29, s32[1]{0:T(128)} %bitcast.19.obs_ref), custom_call_target="tpu_custom_call" | custom-call | tf_op jit(solution)/shard_map/pack/pallas_call | solution.py:122
  3.2 26.5 %all_to_all.20 = f32[1312,1,128]{2,1,0:T(1,128)S(1)} all-to-all(f32[1312,1,128]{2,1,0:T(1,128)S(1)} %bitcast.20), channel_id=1, replica_groups=mesh['member'=4,'space'=8] {'member','space'}, dimensions={0} | all-to-all | bytes 1343488 | tf_op jit(solution)/shard_map/all_to_all | solution.py:371
  29.8 6.3 %pressure.1 = f32[128,128]{1,0:T(8,128)S(1)} custom-call(f32[1312,128]{1,0:T(8,128)S(1)} %bitcast.21), custom_call_target="tpu_custom_call" | custom-call | tf_op jit(solution)/shard_map/pressure/pallas_call | solution.py:122
  36.1 0.0 copy-start.1
  36.1 9.5 %all_to_all.21 = f32[128,1,128]{2,1,0:T(1,128)S(1)} all-to-all(f32[128,1,128]{2,1,0:T(1,128)S(1)} %bitcast.26), channel_id=1, replica_groups=mesh['member'=4,'space'=8] {'member','space'}, dimensions={0} | all-to-all | bytes 131072 | tf_op jit(solution)/shard_map/all_to_all | solution.py:371
  45.6 0.0 copy-done.1
  45.6 0.0 copy-start
  45.6 1.1 %sums.1 = f32[32,8,128]{2,1,0:T(8,128)S(1)} custom-call(f32[128,128]{1,0:T(8,128)S(1)} %bitcast.24, f32[1,128]{1,0:T(1,128)} %bitcast.30, f32[128,128]{1,0:T(8,128)S(1)} %bitcast.27, f32[1,128]{1,0:T(1,128)} %bitcast.31), custom_call_target="tpu_custom_call" | custom-call | tf_op jit(solution)/shard_map/sums/pallas_call | solution.py:122
  46.7 9.9 %all_to_all.22 = f32[32,8,128]{2,1,0:T(8,128)S(1)} all-to-all(f32[32,8,128]{2,1,0:T(8,128)S(1)} %sums.1), channel_id=1, replica_groups=mesh['member'=4,'space'=8] {'member','space'}, dimensions={0} | all-to-all | bytes 262144 | tf_op jit(solution)/shard_map/all_to_all | solution.py:371
  56.6 0.7 broadcast_in_dim.2
  57.3 2.6 %all-to-all-start.3 = ((f32[32,8,128]{2,1,0:T(8,128)}), f32[32,8,128]{2,1,0:T(8,128)S(1)}, u32[]{:S(2)}, u32[]{:S(2)}) async-start(f32[32,8,128]{2,1,0:T(8,128)} %broadcast_in_dim.2), calls=%async_computation.3 | async-start | bytes 262144 | tf_op jit(solution)/shard_map/all_to_all | solution.py:371
  59.9 8.2 %all-to-all-done.3.sums_ref = f32[32,8,128]{2,1,0:T(8,128)S(1)} async-done(((f32[32,8,128]{2,1,0:T(8,128)}), f32[32,8,128]{2,1,0:T(8,128)S(1)}, u32[]{:S(2)}, u32[]{:S(2)}) %all-to-all-start.3) | async-done | bytes 131104 | tf_op jit(solution)/shard_map/all_to_all | solution.py:371
  68.0 0.0 copy-done
  68.0 5.6 %update.1 = f32[1024,128]{1,0:T(8,128)} custom-call(f32[32,8,128]{2,1,0:T(8,128)S(1)} %all-to-all-done.3.sums_ref, f32[1024,128]{1,0:T(8,128)S(1)} %bitcast.23), custom_call_target="tpu_custom_call" | custom-call | tf_op jit(solution)/shard_map/update/pallas_call | solution.py:122
  73.6 0.6 copy.14
  (1 shorter events, 0.0 us)
Async XLA Ops:
  36.1 9.5 %copy-start.1 = (f32[128,1,1,128]{3,2,1,0:T(1,128)S(1)}, f32[128,1,1,128]{3,2,1,0:T(1,128)}, u32[]{:S(2)}) copy-start(f32[128,1,1,128]{3,2,1,0:T(1,128)} %param.10) | copy-start | bytes 196612
  45.6 22.4 %copy-start = (f32[128,2,4,128]{3,2,1,0:T(4,128)S(1)}, f32[128,2,4,128]{3,2,1,0:T(4,128)}, u32[]{:S(2)}) copy-start(f32[128,2,4,128]{3,2,1,0:T(4,128)} %param.6) | copy-start | bytes 1572868
  57.3 10.7 %all-to-all-start.3 = ((f32[32,8,128]{2,1,0:T(8,128)}), f32[32,8,128]{2,1,0:T(8,128)S(1)}, u32[]{:S(2)}, u32[]{:S(2)}) async-start(f32[32,8,128]{2,1,0:T(8,128)} %broadcast_in_dim.2), calls=%async_computation.3 | async-start | bytes 262144 | tf_op jit(solution)/shard_map/all_to_all | solution.py:371

commit v4 on v3

--- a/solution.py
+++ b/solution.py
@@ -117,13 +117,13 @@
     return (updated.reshape(ensemble.shape), predicted)
 
 
-def vmem_call(kernel, out, scratch, name, *operands, spaces=None):
+def vmem_call(kernel, out, scratch, name, *operands, spaces=None, outs=pl.BlockSpec(memory_space=pltpu.VMEM)):
     specs = [pl.BlockSpec(memory_space=s) for s in spaces or [pltpu.VMEM] * len(operands)]
     return pl.pallas_call(
         kernel,
         out_shape=out,
         in_specs=specs,
-        out_specs=pl.BlockSpec(memory_space=pltpu.VMEM),
+        out_specs=outs,
         scratch_shapes=scratch,
         name=name,
     )(*operands)
@@ -133,22 +133,25 @@
     return pltpu.with_memory_space_constraint(x, pltpu.VMEM)
 
 
-def pack_kernel(field_ref, source_ref, obs_ref, out_ref, sems):
-    devices, rows, _, nz = out_ref.shape
+def pack_kernel(field_ref, source_ref, obs_ref, out_ref, block_ref, rows_ref, sems):
+    devices, _, _, nz = out_ref.shape
     cells, block, n_obs = field_ref.shape[1], source_ref.shape[0], obs_ref.shape[0]
-    copies = [
-        pltpu.make_async_copy(field_ref.at[d], out_ref.at[d, pl.ds(0, cells)], sems.at[d]) for d in range(devices)
-    ]
-    for copy in copies:
-        copy.start()
-    source = source_ref[...]
-    picks = [jnp.full((1, 1, nz), obs_ref[o].astype(jnp.float32)) for o in range(n_obs)]
+    fields = pltpu.make_async_copy(field_ref, out_ref.at[:, pl.ds(0, cells)], sems.at[0])
+    source = pltpu.make_async_copy(source_ref, block_ref, sems.at[1])
+    rows = pltpu.make_async_copy(obs_ref, rows_ref, sems.at[2])
+    rows.start()
+    source.start()
+    fields.start()
+    rows.wait()
+    for o in range(n_obs):
+        pick = jnp.full((1, 1, nz), rows_ref[o].astype(jnp.float32))
+        for d in range(devices):
+            out_ref[d, pl.ds(cells + block + o, 1)] = pick
+    source.wait()
+    held = block_ref[...]
     for d in range(devices):
-        out_ref[d, pl.ds(cells, block)] = source
-        for o in range(n_obs):
-            out_ref[d, pl.ds(cells + block + o, 1)] = picks[o]
-    for copy in copies:
-        copy.wait()
+        out_ref[d, pl.ds(cells, block)] = held
+    fields.wait()
 
 
 def total(acc):
@@ -313,7 +316,16 @@
         out_ref[d, held : 2 * held, :] = cross[d * held : (d + 1) * held, :]
 
 
-def update_kernel(sums_ref, field_ref, out_ref, a_ref, c_ref, *, devices):
+def spread_kernel(parts_ref, out_ref):
+    devices = parts_ref.shape[0]
+    own = jnp.sum(parts_ref[...], axis=0)
+    for d in range(devices):
+        out_ref[d] = own
+
+
+def update_kernel(sums_ref, field_ref, found_ref, out_ref, predicted_ref, a_ref, c_ref, sem, *, devices):
+    predicted = pltpu.make_async_copy(found_ref, predicted_ref, sem)
+    predicted.start()
     members = sums_ref.shape[2]
     held = members // devices
     tile = 8
@@ -365,6 +377,7 @@
         anomaly = field - jnp.sum(field, axis=0, keepdims=True) / members
         moved = lax.dot_general(weights, anomaly, by_first, precision=HIGHEST, preferred_element_type=jnp.float32)
         out_ref[pl.ds(c, members, stride=cells), :] = field + moved
+    predicted.wait()
 
 
 def exchange(x):
@@ -383,12 +396,16 @@
     packed = vmem_call(
         pack_kernel,
         pltpu.VMEM((devices, rows, 1, nz), jnp.float32),
-        [pltpu.SemaphoreType.DMA((devices,))],
+        [
+            pltpu.VMEM((block, 1, nz), jnp.float32),
+            pltpu.SMEM((n_obs,), jnp.int32),
+            pltpu.SemaphoreType.DMA((3,)),
+        ],
         "pack",
         ensemble.reshape(devices, held * block, 1, nz),
         source.reshape(block, 1, nz),
         obs_rows.reshape(-1),
-        spaces=[pl.ANY, pltpu.VMEM, pltpu.SMEM],
+        spaces=[pl.ANY] * 3,
     )
     got = exchange(packed.reshape(devices * rows, 1, nz)).reshape(devices * rows, nz)
     nx, ny = n_s * bx, n_m * by
@@ -412,17 +429,22 @@
         near(obs_noise.reshape(members, -1)),
         obs_var.reshape(1, -1),
     )
-    own = jnp.sum(exchange(sums), axis=0, keepdims=True)
-    gathered = exchange(jnp.broadcast_to(own, sums.shape))
-    updated = vmem_call(
+    own = vmem_call(spread_kernel, pltpu.VMEM(sums.shape, jnp.float32), [], "spread", near(exchange(sums)))
+    gathered = exchange(own)
+    updated, predicted = vmem_call(
         functools.partial(update_kernel, devices=devices),
-        jax.ShapeDtypeStruct((members * block, nz), jnp.float32),
-        [pltpu.VMEM((members, members), jnp.float32)] * 2,
+        [
+            jax.ShapeDtypeStruct((members * block, nz), jnp.float32),
+            jax.ShapeDtypeStruct((members, n_obs * nz), jnp.float32),
+        ],
+        [pltpu.VMEM((members, members), jnp.float32)] * 2 + [pltpu.SemaphoreType.DMA],
         "update",
         near(gathered),
         near(ensemble.reshape(members * block, nz)),
-    )
-    return (updated.reshape(ensemble.shape), returned.reshape(members, 1, 1, n_obs * nz))
+        near(returned.reshape(members, n_obs * nz)),
+        outs=[pl.BlockSpec(memory_space=pltpu.VMEM), pl.BlockSpec(memory_space=pl.ANY)],
+    )
+    return (updated.reshape(ensemble.shape), predicted.reshape(members, 1, 1, n_obs * nz))
 
 
 def local(ensemble, *rest):

time: 74.7 us -> 71.5 us (0.957)
  blocking collectives: 45.9 us -> 55.7 us
  waiting for transfers between devices: 8.16 us -> 0 us
  starting transfers between devices: 2.58 us -> 0 us
  local copies, waits for them, and re-layouts: 1.31 us -> 0.01 us
  Pallas kernels: 14.9 us -> 14.1 us
    all_to_all x3 -> x4, blocking collectives: 45.9 us -> 55.7 us  [exchange(): return lax.all_to_all(x, AXES, split_axis=0, concat_axis=0, tiled=True)]
    all_to_all x1 -> x0, waiting for transfers between devices: 8.16 us -> none  [exchange(): return lax.all_to_all(x, AXES, split_axis=0, concat_axis=0, tiled=True)]
    all_to_all x1 -> x0, starting transfers between devices: 2.58 us -> none  [exchange(): return lax.all_to_all(x, AXES, split_axis=0, concat_axis=0, tiled=True)]
    pallas_call x4 -> x5, Pallas kernels: 14.9 us -> 14.1 us  [vmem_call(): pl.pallas_call(kernel, out_shape=out, in_specs=specs, out_specs=outs, scr...]
  transfers between devices with their start and end apart: 1 -> 0, of which waited for: 1 -> 0; matrix products, arithmetic and copies ran while one was open for 0% -> 0% of each run, Pallas kernels for 0% -> 0%
where the time goes in v4:
time: 71.5 us; the launch traced here: 71.2 us
  blocking collectives  55.7 us (78%)
  Pallas kernels  14.1 us (20%)
  between operations  1.31 us (2%)
    all_to_all x4, blocking collectives, exchange(): return lax.all_to_all(x, AXES, split_axis=0, concat_axis=0, tiled=True)  55.7 us
    pallas_call x5, Pallas kernels, vmem_call(): pl.pallas_call(kernel, out_shape=out, in_specs=specs, out_specs=outs, scr...  14.1 us

profile of v4, /device:TPU:0, one launch (start us, length us, event | category | flops | bytes accessed | tf_op | source)
XLA Modules:
  0.0 71.2 jit_solution(17407225079430666563)
XLA Ops:
  1.3 1.1 %pack.1 = f32[32,41,1,128]{3,2,1,0:T(1,128)S(1)} custom-call(f32[32,32,1,128]{3,2,1,0:T(1,128)} %bitcast.22, f32[8,1,128]{2,1,0:T(1,128)} %bitcast.28, s32[1]{0:T(128)} %bitcast.19.obs_ref), custom_call_target="tpu_custom_call" | custom-call | tf_op jit(solution)/shard_map/pack/pallas_call | solution.py:122
  2.4 26.5 %all_to_all.20 = f32[1312,1,128]{2,1,0:T(1,128)S(1)} all-to-all(f32[1312,1,128]{2,1,0:T(1,128)S(1)} %bitcast.20), channel_id=1, replica_groups=mesh['member'=4,'space'=8] {'member','space'}, dimensions={0} | all-to-all | bytes 1343488 | tf_op jit(solution)/shard_map/all_to_all | solution.py:384
  28.9 6.3 %pressure.1 = f32[128,128]{1,0:T(8,128)S(1)} custom-call(f32[1312,128]{1,0:T(8,128)S(1)} %bitcast.21), custom_call_target="tpu_custom_call" | custom-call | tf_op jit(solution)/shard_map/pressure/pallas_call | solution.py:122
  35.2 0.0 copy-start.1
  35.2 9.5 %all_to_all.21 = f32[128,1,128]{2,1,0:T(1,128)S(1)} all-to-all(f32[128,1,128]{2,1,0:T(1,128)S(1)} %bitcast.26), channel_id=1, replica_groups=mesh['member'=4,'space'=8] {'member','space'}, dimensions={0} | all-to-all | bytes 131072 | tf_op jit(solution)/shard_map/all_to_all | solution.py:384
  44.7 0.0 copy-done.1
  44.7 0.0 copy-start
  44.7 1.1 %sums.1 = f32[32,8,128]{2,1,0:T(8,128)S(1)} custom-call(f32[128,128]{1,0:T(8,128)S(1)} %bitcast.24, f32[1,128]{1,0:T(1,128)} %bitcast.29, f32[128,128]{1,0:T(8,128)S(1)} %bitcast.27, f32[1,128]{1,0:T(1,128)} %bitcast.30), custom_call_target="tpu_custom_call" | custom-call | tf_op jit(solution)/shard_map/sums/pallas_call | solution.py:122
  45.8 9.9 %all_to_all.22.parts_ref = f32[32,8,128]{2,1,0:T(8,128)S(1)} all-to-all(f32[32,8,128]{2,1,0:T(8,128)S(1)} %sums.1), channel_id=1, replica_groups=mesh['member'=4,'space'=8] {'member','space'}, dimensions={0} | all-to-all | bytes 262144 | tf_op jit(solution)/shard_map/all_to_all | solution.py:384
  55.8 9.9 %all_to_all.23.sums_ref = f32[32,8,128]{2,1,0:T(8,128)S(1)} all-to-all(f32[32,8,128]{2,1,0:T(8,128)S(1)} %spread.1), channel_id=1, replica_groups=mesh['member'=4,'space'=8] {'member','space'}, dimensions={0} | all-to-all | bytes 262144 | tf_op jit(solution)/shard_map/all_to_all | solution.py:384
  65.6 0.0 copy-done
  65.6 5.6 %update.1 = (f32[1024,128]{1,0:T(8,128)}, f32[128,128]{1,0:T(8,128)}) custom-call(f32[32,8,128]{2,1,0:T(8,128)S(1)} %all_to_all.23.sums_ref, f32[1024,128]{1,0:T(8,128)S(1)} %bitcast.23, f32[128,128]{1,0:T(8,128)S(1)} %bitcast.25), custom_call_target="tpu_custom_call" | custom-call | tf_op jit(solution)/shard_map/update/pallas_call | solution.py:122
  (1 shorter events, 0.0 us)
Async XLA Ops:
  35.2 9.5 %copy-start.1 = (f32[128,1,1,128]{3,2,1,0:T(1,128)S(1)}, f32[128,1,1,128]{3,2,1,0:T(1,128)}, u32[]{:S(2)}) copy-start(f32[128,1,1,128]{3,2,1,0:T(1,128)} %param.10) | copy-start | bytes 196612
  44.7 20.9 %copy-start = (f32[128,2,4,128]{3,2,1,0:T(4,128)S(1)}, f32[128,2,4,128]{3,2,1,0:T(4,128)}, u32[]{:S(2)}) copy-start(f32[128,2,4,128]{3,2,1,0:T(4,128)} %param.6) | copy-start | bytes 1572868

commit v5 on v4

--- a/solution.py
+++ b/solution.py
@@ -8,6 +8,8 @@
 from jax.sharding import PartitionSpec as P
 
 ITERS = 4
+TILE = 8
+UNROLL = 4
 AXES = ("member", "space")
 HIGHEST = lax.Precision.HIGHEST
 
@@ -158,7 +160,7 @@
     return jnp.sum(jnp.sum(acc, axis=0, keepdims=True), axis=1, keepdims=True)
 
 
-def pressure_kernel(g_ref, out_ref, e_ref, fx_ref, fy_ref, fz_ref, bd_ref, p_ref, r_ref, q_ref, x_ref, acc_ref, norm_ref, *, dims):
+def pressure_kernel(g_ref, out_ref, e_ref, fx_ref, fy_ref, fz_ref, mid_ref, p_ref, r_ref, q_ref, x_ref, acc_ref, norm_ref, *, dims):
     n_m, n_s, held, bx, by, n_obs = dims
     nx, ny = n_s * bx, n_m * by
     nz = g_ref.shape[1]
@@ -168,18 +170,23 @@
     lane = lax.broadcasted_iota(jnp.int32, plane, 1)
     sub = lax.broadcasted_iota(jnp.int32, plane, 0)
 
-    def at(j, x):
-        return pl.ds(pl.multiple_of((j * nx + x) * ny, ny), ny)
+    def at(j, x, shift=0):
+        start = pl.multiple_of((j * nx + x) * ny, ny)
+        return pl.ds(start + (TILE + shift), ny)
 
     def member(j):
         return pl.ds(pl.multiple_of(j * ny, ny), ny)
 
-    def for_members(fn):
+    def for_members(fn, unroll=1):
         def body(j, carry):
             fn(j)
             return carry
 
-        lax.fori_loop(0, held, body, 0)
+        lax.fori_loop(0, held, body, 0, unroll=unroll)
+
+    for ref in (p_ref, fy_ref):
+        for edge in (0, TILE + held * nx * ny):
+            ref[pl.ds(edge, TILE), :] = jnp.zeros((TILE, nz), jnp.float32)
 
     for m in range(n_m):
         for s in range(n_s):
@@ -187,13 +194,11 @@
             for a in range(bx):
                 x = s * bx + a
                 for j in range(held):
-                    e_ref[pl.ds((j * nx + x) * ny + m * by, by), :] = g_ref[
+                    e_ref[pl.ds(TILE + (j * nx + x) * ny + m * by, by), :] = g_ref[
                         pl.ds(base + j * block + a * by, by), :
                     ]
-                x_ref[pl.ds(x * ny + m * by, by), :] = g_ref[pl.ds(base + held * block + a * by, by), :]
-
-    edge_z = (lane == 0).astype(jnp.float32) + (lane == nz - 1).astype(jnp.float32)
-    edge_y = (sub == 0).astype(jnp.float32) + (sub == ny - 1).astype(jnp.float32)
+                x_ref[pl.ds(TILE + x * ny + m * by, by), :] = g_ref[pl.ds(base + held * block + a * by, by), :]
+
     norm0 = jnp.zeros(plane, jnp.float32)
     for x in range(nx):
         v = x_ref[at(0, x), :]
@@ -204,64 +209,73 @@
     norm0 = jnp.broadcast_to(total(norm0), plane)
     for j in range(held):
         norm_ref[member(j), :] = norm0
+    x_ref[...] = jnp.zeros(x_ref.shape, jnp.float32)
+
+    edge_z = (lane == 0).astype(jnp.float32) + (lane == nz - 1).astype(jnp.float32)
+    edge_y = (sub == 0).astype(jnp.float32) + (sub == ny - 1).astype(jnp.float32)
 
     def faces(j):
-        before = None
+        e = jnp.exp(-e_ref[at(j, 0), :])
+        fx = None
         for x in range(nx):
-            e = jnp.exp(-e_ref[at(j, x), :])
-            if before is not None:
-                fx_ref[at(j, x), :] = 2.0 / (e + before)
-            fy_ref[at(j, x), :] = jnp.where(sub > 0, 2.0 / (e + pltpu.roll(e, 1, 0)), 0.0)
-            fz_ref[at(j, x), :] = jnp.where(lane > 0, 2.0 / (e + pltpu.roll(e, 1, 1)), 0.0)
+            fy = jnp.where(sub > 0, 2.0 / (e + pltpu.roll(e, 1, 0)), 0.0)
+            fz = jnp.where(lane > 0, 2.0 / (e + pltpu.roll(e, 1, 1)), 0.0)
+            fy_ref[at(j, x), :] = fy
+            fz_ref[at(j, x), :] = fz
+            mid = (fy + pltpu.roll(fy, ny - 1, 0)) + (fz + pltpu.roll(fz, nz - 1, 1))
             ends = edge_y + edge_z
             if x == 0 or x == nx - 1:
                 ends = ends + 1.0
-            bd_ref[at(j, x), :] = ends / e
-            before = e
+            mid = mid + ends / e
+            if fx is not None:
+                mid = mid + fx
+            if x + 1 < nx:
+                after = jnp.exp(-e_ref[at(j, x + 1), :])
+                fx = 2.0 / (e + after)
+                fx_ref[at(j, x + 1), :] = fx
+                mid = mid + fx
+                e = after
+            mid_ref[at(j, x), :] = mid
 
     for_members(faces)
 
-    def along_z(j):
+    def along_z(j, x, v):
+        f = fz_ref[at(j, x), :]
+        q_ref[at(j, x), :] = f * pltpu.roll(v, 1, 1) + pltpu.roll(f * v, nz - 1, 1)
+
+    def start(j):
         for x in range(nx):
-            v = p_ref[at(j, x), :]
-            gz = fz_ref[at(j, x), :] * (v - pltpu.roll(v, 1, 1))
-            q_ref[at(j, x), :] = gz - pltpu.roll(gz, nz - 1, 1)
+            along_z(j, x, p_ref[at(j, x), :])
 
     def apply(j):
         acc = jnp.zeros(plane, jnp.float32)
+        before, fx = None, None
         v = p_ref[at(j, 0), :]
-        gx = None
         for x in range(nx):
-            gy = fy_ref[at(j, x), :] * (v - pltpu.roll(v, 1, 0))
-            image = q_ref[at(j, x), :] + bd_ref[at(j, x), :] * v
-            image = image + (gy - pltpu.roll(gy, ny - 1, 0))
-            if gx is not None:
-                image = image + gx
+            image = mid_ref[at(j, x), :] * v - q_ref[at(j, x), :]
+            image = image - fy_ref[at(j, x), :] * p_ref[at(j, x, -1), :]
+            image = image - fy_ref[at(j, x, 1), :] * p_ref[at(j, x, 1), :]
+            if x > 0:
+                image = image - fx * before
             if x + 1 < nx:
                 after = p_ref[at(j, x + 1), :]
-                gx = fx_ref[at(j, x + 1), :] * (after - v)
-                image = image - gx
+                fx = fx_ref[at(j, x + 1), :]
+                image = image - fx * after
             q_ref[at(j, x), :] = image
             acc = acc + v * image
             if x + 1 < nx:
-                v = after
+                before, v = v, after
         acc_ref[member(j), :] = acc
 
     def totals():
         return [jnp.broadcast_to(total(acc_ref[member(j), :]), plane) for j in range(held)]
 
     def multiply():
-        for_members(along_z)
         for_members(apply)
         for j, dot in enumerate(totals()):
             acc_ref[member(j), :] = norm_ref[member(j), :] / dot
 
     def move(j):
-        step = acc_ref[member(j), :]
-        for x in range(nx):
-            x_ref[at(j, x), :] = x_ref[at(j, x), :] + step * p_ref[at(j, x), :]
-
-    def move_and_leave(j):
         step = acc_ref[member(j), :]
         acc = jnp.zeros(plane, jnp.float32)
         for x in range(nx):
@@ -274,21 +288,22 @@
     def turn(j):
         ratio = acc_ref[member(j), :]
         for x in range(nx):
-            p_ref[at(j, x), :] = r_ref[at(j, x), :] + ratio * p_ref[at(j, x), :]
+            v = r_ref[at(j, x), :] + ratio * p_ref[at(j, x), :]
+            p_ref[at(j, x), :] = v
+            along_z(j, x, v)
 
     def one(iteration, carry):
         multiply()
-        for_members(move_and_leave)
+        for_members(move)
         for j, norm in enumerate(totals()):
             acc_ref[member(j), :] = norm / norm_ref[member(j), :]
             norm_ref[member(j), :] = norm
-        for_members(turn)
+        for_members(turn, UNROLL)
         return carry
 
-    x_ref[...] = jnp.zeros(x_ref.shape, jnp.float32)
+    for_members(start, UNROLL)
     lax.fori_loop(0, ITERS - 1, one, 0)
     multiply()
-    for_members(move)
 
     for m in range(n_m):
         for s in range(n_s):
@@ -297,7 +312,10 @@
                 picked = g_ref[pl.ds(peer * rows + (held + 1) * block + o, 1), :].astype(jnp.int32)[0, 0]
                 cell = (s * bx + picked // by) * ny + m * by + picked % by
                 for j in range(held):
-                    out_ref[pl.ds((peer * held + j) * n_obs + o, 1), :] = x_ref[pl.ds(j * nx * ny + cell, 1), :]
+                    row = pl.ds(TILE + j * nx * ny + cell, 1)
+                    out_ref[pl.ds((peer * held + j) * n_obs + o, 1), :] = (
+                        x_ref[row, :] + acc_ref[pl.ds(j * ny, 1), :] * p_ref[row, :]
+                    )
 
 
 def sums_kernel(pred_ref, values_ref, noise_ref, var_ref, out_ref, *, devices):
@@ -409,7 +427,7 @@
     )
     got = exchange(packed.reshape(devices * rows, 1, nz)).reshape(devices * rows, nz)
     nx, ny = n_s * bx, n_m * by
-    field = pltpu.VMEM((held * nx * ny, nz), jnp.float32)
+    field = pltpu.VMEM((held * nx * ny + 2 * TILE, nz), jnp.float32)
     plane = pltpu.VMEM((held * ny, nz), jnp.float32)
     picked = vmem_call(
         functools.partial(pressure_kernel, dims=(n_m, n_s, held, bx, by, n_obs)),

time: 71.5 us -> 70.3 us (0.983)
  Pallas kernels: 14.1 us -> 13 us
    pallas_call x5, Pallas kernels: 14.1 us -> 13 us  [vmem_call(): pl.pallas_call(kernel, out_shape=out, in_specs=specs, out_specs=outs, scr...]
where the time goes in v5:
time: 70.3 us; the launch traced here: 70.1 us
  blocking collectives  55.7 us (79%)
  Pallas kernels  13 us (18%)
  between operations  1.31 us (2%)
    all_to_all x4, blocking collectives, exchange(): return lax.all_to_all(x, AXES, split_axis=0, concat_axis=0, tiled=True)  55.7 us
    pallas_call x5, Pallas kernels, vmem_call(): pl.pallas_call(kernel, out_shape=out, in_specs=specs, out_specs=outs, scr...  13 us

profile of v5, /device:TPU:0, one launch (start us, length us, event | category | flops | bytes accessed | tf_op | source)
XLA Modules:
  0.0 70.1 jit_solution(10487007195311761852)
XLA Ops:
  1.3 1.1 %pack.1 = f32[32,41,1,128]{3,2,1,0:T(1,128)S(1)} custom-call(f32[32,32,1,128]{3,2,1,0:T(1,128)} %bitcast.22, f32[8,1,128]{2,1,0:T(1,128)} %bitcast.28, s32[1]{0:T(128)} %bitcast.19.obs_ref), custom_call_target="tpu_custom_call" | custom-call | tf_op jit(solution)/shard_map/pack/pallas_call | solution.py:124
  2.4 26.5 %all_to_all.20 = f32[1312,1,128]{2,1,0:T(1,128)S(1)} all-to-all(f32[1312,1,128]{2,1,0:T(1,128)S(1)} %bitcast.20), channel_id=1, replica_groups=mesh['member'=4,'space'=8] {'member','space'}, dimensions={0} | all-to-all | bytes 1343488 | tf_op jit(solution)/shard_map/all_to_all | solution.py:402
  28.9 5.2 %pressure.1 = f32[128,128]{1,0:T(8,128)S(1)} custom-call(f32[1312,128]{1,0:T(8,128)S(1)} %bitcast.21), custom_call_target="tpu_custom_call" | custom-call | tf_op jit(solution)/shard_map/pressure/pallas_call | solution.py:124
  34.1 0.0 copy-start.1
  34.1 9.5 %all_to_all.21 = f32[128,1,128]{2,1,0:T(1,128)S(1)} all-to-all(f32[128,1,128]{2,1,0:T(1,128)S(1)} %bitcast.26), channel_id=1, replica_groups=mesh['member'=4,'space'=8] {'member','space'}, dimensions={0} | all-to-all | bytes 131072 | tf_op jit(solution)/shard_map/all_to_all | solution.py:402
  43.6 0.0 copy-done.1
  43.6 0.0 copy-start
  43.6 1.1 %sums.1 = f32[32,8,128]{2,1,0:T(8,128)S(1)} custom-call(f32[128,128]{1,0:T(8,128)S(1)} %bitcast.24, f32[1,128]{1,0:T(1,128)} %bitcast.29, f32[128,128]{1,0:T(8,128)S(1)} %bitcast.27, f32[1,128]{1,0:T(1,128)} %bitcast.30), custom_call_target="tpu_custom_call" | custom-call | tf_op jit(solution)/shard_map/sums/pallas_call | solution.py:124
  44.7 9.9 %all_to_all.22.parts_ref = f32[32,8,128]{2,1,0:T(8,128)S(1)} all-to-all(f32[32,8,128]{2,1,0:T(8,128)S(1)} %sums.1), channel_id=1, replica_groups=mesh['member'=4,'space'=8] {'member','space'}, dimensions={0} | all-to-all | bytes 262144 | tf_op jit(solution)/shard_map/all_to_all | solution.py:402
  54.6 9.9 %all_to_all.23.sums_ref = f32[32,8,128]{2,1,0:T(8,128)S(1)} all-to-all(f32[32,8,128]{2,1,0:T(8,128)S(1)} %spread.1), channel_id=1, replica_groups=mesh['member'=4,'space'=8] {'member','space'}, dimensions={0} | all-to-all | bytes 262144 | tf_op jit(solution)/shard_map/all_to_all | solution.py:402
  64.5 0.0 copy-done
  64.5 5.6 %update.1 = (f32[1024,128]{1,0:T(8,128)}, f32[128,128]{1,0:T(8,128)}) custom-call(f32[32,8,128]{2,1,0:T(8,128)S(1)} %all_to_all.23.sums_ref, f32[1024,128]{1,0:T(8,128)S(1)} %bitcast.23, f32[128,128]{1,0:T(8,128)S(1)} %bitcast.25), custom_call_target="tpu_custom_call" | custom-call | tf_op jit(solution)/shard_map/update/pallas_call | solution.py:124
  (1 shorter events, 0.0 us)
Async XLA Ops:
  34.1 9.5 %copy-start.1 = (f32[128,1,1,128]{3,2,1,0:T(1,128)S(1)}, f32[128,1,1,128]{3,2,1,0:T(1,128)}, u32[]{:S(2)}) copy-start(f32[128,1,1,128]{3,2,1,0:T(1,128)} %param.10) | copy-start | bytes 196612
  43.6 20.9 %copy-start = (f32[128,2,4,128]{3,2,1,0:T(4,128)S(1)}, f32[128,2,4,128]{3,2,1,0:T(4,128)}, u32[]{:S(2)}) copy-start(f32[128,2,4,128]{3,2,1,0:T(4,128)} %param.6) | copy-start | bytes 1572868

commit v6 on v5

--- a/solution.py
+++ b/solution.py
@@ -9,7 +9,6 @@
 
 ITERS = 4
 TILE = 8
-UNROLL = 4
 AXES = ("member", "space")
 HIGHEST = lax.Precision.HIGHEST
 
@@ -177,12 +176,12 @@
     def member(j):
         return pl.ds(pl.multiple_of(j * ny, ny), ny)
 
-    def for_members(fn, unroll=1):
+    def for_members(fn):
         def body(j, carry):
             fn(j)
             return carry
 
-        lax.fori_loop(0, held, body, 0, unroll=unroll)
+        lax.fori_loop(0, held, body, 0)
 
     for ref in (p_ref, fy_ref):
         for edge in (0, TILE + held * nx * ny):
@@ -239,15 +238,15 @@
 
     for_members(faces)
 
-    def along_z(j, x, v):
-        f = fz_ref[at(j, x), :]
-        q_ref[at(j, x), :] = f * pltpu.roll(v, 1, 1) + pltpu.roll(f * v, nz - 1, 1)
-
-    def start(j):
+    def turn(j, ratio):
         for x in range(nx):
-            along_z(j, x, p_ref[at(j, x), :])
-
-    def apply(j):
+            v = r_ref[at(j, x), :] + ratio * p_ref[at(j, x), :]
+            p_ref[at(j, x), :] = v
+            f = fz_ref[at(j, x), :]
+            q_ref[at(j, x), :] = f * pltpu.roll(v, 1, 1) + pltpu.roll(f * v, nz - 1, 1)
+            yield
+
+    def apply(j, dots):
         acc = jnp.zeros(plane, jnp.float32)
         before, fx = None, None
         v = p_ref[at(j, 0), :]
@@ -265,45 +264,62 @@
             acc = acc + v * image
             if x + 1 < nx:
                 before, v = v, after
-        acc_ref[member(j), :] = acc
-
-    def totals():
-        return [jnp.broadcast_to(total(acc_ref[member(j), :]), plane) for j in range(held)]
-
-    def multiply():
-        for_members(apply)
-        for j, dot in enumerate(totals()):
-            acc_ref[member(j), :] = norm_ref[member(j), :] / dot
-
-    def move(j):
-        step = acc_ref[member(j), :]
+            yield
+        dots[j] = acc
+
+    def move(j, step, norms):
         acc = jnp.zeros(plane, jnp.float32)
         for x in range(nx):
             x_ref[at(j, x), :] = x_ref[at(j, x), :] + step * p_ref[at(j, x), :]
             res = r_ref[at(j, x), :] - step * q_ref[at(j, x), :]
             r_ref[at(j, x), :] = res
             acc = acc + res * res
-        acc_ref[member(j), :] = acc
-
-    def turn(j):
-        ratio = acc_ref[member(j), :]
-        for x in range(nx):
-            v = r_ref[at(j, x), :] + ratio * p_ref[at(j, x), :]
-            p_ref[at(j, x), :] = v
-            along_z(j, x, v)
+            yield
+        norms[j] = acc
+
+    def together(*stages):
+        stages = list(stages)
+        while stages:
+            stages = [stage for stage in stages if next(stage, stage) is not stage]
+
+    def spread_total(acc):
+        return jnp.broadcast_to(total(acc), plane)
+
+    def steps_of(dots):
+        return {j: norm_ref[member(j), :] / spread_total(dot) for j, dot in dots.items()}
+
+    def ratios_of(norms):
+        ratios = {}
+        for j, norm in norms.items():
+            norm = spread_total(norm)
+            ratios[j] = norm / norm_ref[member(j), :]
+            norm_ref[member(j), :] = norm
+        return ratios
+
+    ahead, behind = range(held // 2), range(held // 2, held)
+
+    def open_stage():
+        dots = {}
+        together(*[apply(j, dots) for j in ahead], *[turn(j, acc_ref[member(j), :]) for j in behind])
+        return steps_of(dots)
 
     def one(iteration, carry):
-        multiply()
-        for_members(move)
-        for j, norm in enumerate(totals()):
-            acc_ref[member(j), :] = norm / norm_ref[member(j), :]
-            norm_ref[member(j), :] = norm
-        for_members(turn, UNROLL)
+        steps, dots, norms = open_stage(), {}, {}
+        together(*[apply(j, dots) for j in behind], *[move(j, steps[j], norms) for j in ahead])
+        ratios, steps, norms = ratios_of(norms), steps_of(dots), {}
+        together(*[turn(j, ratios[j]) for j in ahead], *[move(j, steps[j], norms) for j in behind])
+        for j, ratio in ratios_of(norms).items():
+            acc_ref[member(j), :] = ratio
         return carry
 
-    for_members(start, UNROLL)
+    acc_ref[...] = jnp.zeros(acc_ref.shape, jnp.float32)
+    together(*[turn(j, acc_ref[member(j), :]) for j in ahead])
     lax.fori_loop(0, ITERS - 1, one, 0)
-    multiply()
+    steps, dots = open_stage(), {}
+    together(*[apply(j, dots) for j in behind])
+    steps.update(steps_of(dots))
+    for j, step in steps.items():
+        acc_ref[member(j), :] = step
 
     for m in range(n_m):
         for s in range(n_s):

time: 70.3 us -> 69.2 us (0.984)
  Pallas kernels: 13 us -> 11.9 us
    pallas_call x5, Pallas kernels: 13 us -> 11.9 us  [vmem_call(): pl.pallas_call(kernel, out_shape=out, in_specs=specs, out_specs=outs, scr...]
where the time goes in v6:
time: 69.2 us; the launch traced here: 68.9 us
  blocking collectives  55.7 us (80%)
  Pallas kernels  11.9 us (17%)
  between operations  1.31 us (2%)
    all_to_all x4, blocking collectives, exchange(): return lax.all_to_all(x, AXES, split_axis=0, concat_axis=0, tiled=True)  55.7 us
    pallas_call x5, Pallas kernels, vmem_call(): pl.pallas_call(kernel, out_shape=out, in_specs=specs, out_specs=outs, scr...  11.9 us

profile of v6, /device:TPU:0, one launch (start us, length us, event | category | flops | bytes accessed | tf_op | source)
XLA Modules:
  0.0 68.9 jit_solution(9922247542338502247)
XLA Ops:
  1.3 1.1 %pack.1 = f32[32,41,1,128]{3,2,1,0:T(1,128)S(1)} custom-call(f32[32,32,1,128]{3,2,1,0:T(1,128)} %bitcast.22, f32[8,1,128]{2,1,0:T(1,128)} %bitcast.28, s32[1]{0:T(128)} %bitcast.19.obs_ref), custom_call_target="tpu_custom_call" | custom-call | tf_op jit(solution)/shard_map/pack/pallas_call | solution.py:123
  2.4 26.5 %all_to_all.20 = f32[1312,1,128]{2,1,0:T(1,128)S(1)} all-to-all(f32[1312,1,128]{2,1,0:T(1,128)S(1)} %bitcast.20), channel_id=1, replica_groups=mesh['member'=4,'space'=8] {'member','space'}, dimensions={0} | all-to-all | bytes 1343488 | tf_op jit(solution)/shard_map/all_to_all | solution.py:418
  28.9 4.0 %pressure.1 = f32[128,128]{1,0:T(8,128)S(1)} custom-call(f32[1312,128]{1,0:T(8,128)S(1)} %bitcast.21), custom_call_target="tpu_custom_call" | custom-call | tf_op jit(solution)/shard_map/pressure/pallas_call | solution.py:123
  33.0 0.0 copy-start.1
  33.0 9.5 %all_to_all.21 = f32[128,1,128]{2,1,0:T(1,128)S(1)} all-to-all(f32[128,1,128]{2,1,0:T(1,128)S(1)} %bitcast.26), channel_id=1, replica_groups=mesh['member'=4,'space'=8] {'member','space'}, dimensions={0} | all-to-all | bytes 131072 | tf_op jit(solution)/shard_map/all_to_all | solution.py:418
  42.5 0.0 copy-done.1
  42.5 0.0 copy-start
  42.5 1.1 %sums.1 = f32[32,8,128]{2,1,0:T(8,128)S(1)} custom-call(f32[128,128]{1,0:T(8,128)S(1)} %bitcast.24, f32[1,128]{1,0:T(1,128)} %bitcast.29, f32[128,128]{1,0:T(8,128)S(1)} %bitcast.27, f32[1,128]{1,0:T(1,128)} %bitcast.30), custom_call_target="tpu_custom_call" | custom-call | tf_op jit(solution)/shard_map/sums/pallas_call | solution.py:123
  43.6 9.9 %all_to_all.22.parts_ref = f32[32,8,128]{2,1,0:T(8,128)S(1)} all-to-all(f32[32,8,128]{2,1,0:T(8,128)S(1)} %sums.1), channel_id=1, replica_groups=mesh['member'=4,'space'=8] {'member','space'}, dimensions={0} | all-to-all | bytes 262144 | tf_op jit(solution)/shard_map/all_to_all | solution.py:418
  53.5 9.9 %all_to_all.23.sums_ref = f32[32,8,128]{2,1,0:T(8,128)S(1)} all-to-all(f32[32,8,128]{2,1,0:T(8,128)S(1)} %spread.1), channel_id=1, replica_groups=mesh['member'=4,'space'=8] {'member','space'}, dimensions={0} | all-to-all | bytes 262144 | tf_op jit(solution)/shard_map/all_to_all | solution.py:418
  63.4 0.0 copy-done
  63.4 5.6 %update.1 = (f32[1024,128]{1,0:T(8,128)}, f32[128,128]{1,0:T(8,128)}) custom-call(f32[32,8,128]{2,1,0:T(8,128)S(1)} %all_to_all.23.sums_ref, f32[1024,128]{1,0:T(8,128)S(1)} %bitcast.23, f32[128,128]{1,0:T(8,128)S(1)} %bitcast.25), custom_call_target="tpu_custom_call" | custom-call | tf_op jit(solution)/shard_map/update/pallas_call | solution.py:123
  (1 shorter events, 0.0 us)
Async XLA Ops:
  33.0 9.5 %copy-start.1 = (f32[128,1,1,128]{3,2,1,0:T(1,128)S(1)}, f32[128,1,1,128]{3,2,1,0:T(1,128)}, u32[]{:S(2)}) copy-start(f32[128,1,1,128]{3,2,1,0:T(1,128)} %param.10) | copy-start | bytes 196612
  42.5 20.9 %copy-start = (f32[128,2,4,128]{3,2,1,0:T(4,128)S(1)}, f32[128,2,4,128]{3,2,1,0:T(4,128)}, u32[]{:S(2)}) copy-start(f32[128,2,4,128]{3,2,1,0:T(4,128)} %param.6) | copy-start | bytes 1572868

commit v7 on v6

--- a/solution.py
+++ b/solution.py
@@ -159,13 +159,17 @@
     return jnp.sum(jnp.sum(acc, axis=0, keepdims=True), axis=1, keepdims=True)
 
 
-def pressure_kernel(g_ref, out_ref, e_ref, fx_ref, fy_ref, fz_ref, mid_ref, p_ref, r_ref, q_ref, x_ref, acc_ref, norm_ref, *, dims):
+def pressure_kernel(g_ref, values_hbm, noise_hbm, var_hbm, out_ref, aim_ref, scale_ref, values_ref, var_ref, sems, e_ref, fx_ref, fy_ref, fz_ref, mid_ref, p_ref, r_ref, q_ref, x_ref, acc_ref, norm_ref, *, dims):
     n_m, n_s, held, bx, by, n_obs = dims
     nx, ny = n_s * bx, n_m * by
     nz = g_ref.shape[1]
     block = bx * by
     rows = (held + 1) * block + n_obs
     plane = (ny, nz)
+    fetched = ((noise_hbm, aim_ref), (values_hbm, values_ref), (var_hbm, var_ref))
+    fetches = [pltpu.make_async_copy(x, y, sems.at[i]) for i, (x, y) in enumerate(fetched)]
+    for fetch in fetches:
+        fetch.start()
     lane = lax.broadcasted_iota(jnp.int32, plane, 1)
     sub = lax.broadcasted_iota(jnp.int32, plane, 0)
 
@@ -321,6 +325,12 @@
     for j, step in steps.items():
         acc_ref[member(j), :] = step
 
+    for fetch in fetches:
+        fetch.wait()
+    inv_sigma = 1.0 / jnp.sqrt(var_ref[...])
+    scale_ref[...] = inv_sigma
+    aim_ref[...] = aim_ref[...] + values_ref[...] * inv_sigma
+
     for m in range(n_m):
         for s in range(n_s):
             peer = m * n_s + s
@@ -334,14 +344,14 @@
                     )
 
 
-def sums_kernel(pred_ref, values_ref, noise_ref, var_ref, out_ref, *, devices):
+def sums_kernel(pred_ref, aim_ref, scale_ref, out_ref, *, devices):
     members = pred_ref.shape[0]
     held = members // devices
     pred = pred_ref[...]
-    inv_sigma = 1.0 / jnp.sqrt(var_ref[...])
+    inv_sigma = scale_ref[...]
     mean = jnp.sum(pred, axis=0, keepdims=True) / members
     spread = (pred - mean) * inv_sigma
-    misfit = (values_ref[...] - pred) * inv_sigma + noise_ref[...]
+    misfit = aim_ref[...] - pred * inv_sigma
     by_last = (((1,), (1,)), ((), ()))
     gram = lax.dot_general(spread, spread, by_last, precision=HIGHEST, preferred_element_type=jnp.float32)
     cross = lax.dot_general(spread, misfit, by_last, precision=HIGHEST, preferred_element_type=jnp.float32)
@@ -445,12 +455,19 @@
     nx, ny = n_s * bx, n_m * by
     field = pltpu.VMEM((held * nx * ny + 2 * TILE, nz), jnp.float32)
     plane = pltpu.VMEM((held * ny, nz), jnp.float32)
-    picked = vmem_call(
+    observed = n_obs * nz
+    row = pltpu.VMEM((1, observed), jnp.float32)
+    picked, aim, scale = vmem_call(
         functools.partial(pressure_kernel, dims=(n_m, n_s, held, bx, by, n_obs)),
-        pltpu.VMEM((members * n_obs, nz), jnp.float32),
-        [field] * 9 + [plane] * 2,
+        [pltpu.VMEM((members * n_obs, nz), jnp.float32), pltpu.VMEM((members, observed), jnp.float32), row],
+        [row] * 2 + [pltpu.SemaphoreType.DMA((3,))] + [field] * 9 + [plane] * 2,
         "pressure",
         near(got),
+        obs_values.reshape(1, observed),
+        obs_noise.reshape(members, observed),
+        obs_var.reshape(1, observed),
+        spaces=[pltpu.VMEM] + [pl.ANY] * 3,
+        outs=[pl.BlockSpec(memory_space=pltpu.VMEM)] * 3,
     )
     returned = exchange(picked.reshape(members * n_obs, 1, nz))
     sums = vmem_call(
@@ -458,10 +475,9 @@
         pltpu.VMEM((devices, 2 * held, members), jnp.float32),
         [],
         "sums",
-        near(returned.reshape(members, n_obs * nz)),
-        obs_values.reshape(1, -1),
-        near(obs_noise.reshape(members, -1)),
-        obs_var.reshape(1, -1),
+        near(returned.reshape(members, observed)),
+        near(aim),
+        near(scale),
     )
     own = vmem_call(spread_kernel, pltpu.VMEM(sums.shape, jnp.float32), [], "spread", near(exchange(sums)))
     gathered = exchange(own)

time: 69.2 us -> 68.5 us (0.990)
  Pallas kernels: 11.9 us -> 11.2 us
where the time goes in v7:
time: 68.5 us; the launch traced here: 68.3 us
  blocking collectives  55.7 us (81%)
  Pallas kernels  11.2 us (16%)
  between operations  1.31 us (2%)
    all_to_all x4, blocking collectives, exchange(): return lax.all_to_all(x, AXES, split_axis=0, concat_axis=0, tiled=True)  55.7 us
    pallas_call x5, Pallas kernels, vmem_call(): pl.pallas_call(kernel, out_shape=out, in_specs=specs, out_specs=outs, scr...  11.2 us

profile of v7, /device:TPU:0, one launch (start us, length us, event | category | flops | bytes accessed | tf_op | source)
XLA Modules:
  0.0 68.3 jit_solution(10114351128920149048)
XLA Ops:
  1.3 1.1 %pack.1 = f32[32,41,1,128]{3,2,1,0:T(1,128)S(1)} custom-call(f32[32,32,1,128]{3,2,1,0:T(1,128)} %bitcast.22, f32[8,1,128]{2,1,0:T(1,128)} %bitcast.28, s32[1]{0:T(128)} %bitcast.19.obs_ref), custom_call_target="tpu_custom_call" | custom-call | tf_op jit(solution)/shard_map/pack/pallas_call | solution.py:123
  2.4 26.5 %all_to_all.20 = f32[1312,1,128]{2,1,0:T(1,128)S(1)} all-to-all(f32[1312,1,128]{2,1,0:T(1,128)S(1)} %bitcast.21), channel_id=1, replica_groups=mesh['member'=4,'space'=8] {'member','space'}, dimensions={0} | all-to-all | bytes 1343488 | tf_op jit(solution)/shard_map/all_to_all | solution.py:428
  28.9 4.1 %pressure.1 = (f32[128,128]{1,0:T(8,128)S(1)}, f32[128,128]{1,0:T(8,128)S(1)}, f32[1,128]{1,0:T(1,128)S(1)}) custom-call(f32[1312,128]{1,0:T(8,128)S(1)} %bitcast.20, f32[1,128]{1,0:T(1,128)} %bitcast.29, f32[128,128]{1,0:T(8,128)} %bitcast.27, f32[1,128]{1,0:T(1,128)} %bitcast.30), custom_call_target="tpu_custom_call" | custom-call | tf_op jit(solution)/shard_map/pressure/pallas_call | solution.py:123
  33.0 9.5 %all_to_all.21 = f32[128,1,128]{2,1,0:T(1,128)S(1)} all-to-all(f32[128,1,128]{2,1,0:T(1,128)S(1)} %bitcast.26), channel_id=1, replica_groups=mesh['member'=4,'space'=8] {'member','space'}, dimensions={0} | all-to-all | bytes 131072 | tf_op jit(solution)/shard_map/all_to_all | solution.py:428
  42.5 0.0 copy-start
  42.5 0.4 sums.1
  42.9 9.9 %all_to_all.22.parts_ref = f32[32,8,128]{2,1,0:T(8,128)S(1)} all-to-all(f32[32,8,128]{2,1,0:T(8,128)S(1)} %sums.1), channel_id=1, replica_groups=mesh['member'=4,'space'=8] {'member','space'}, dimensions={0} | all-to-all | bytes 262144 | tf_op jit(solution)/shard_map/all_to_all | solution.py:428
  52.8 9.9 %all_to_all.23.sums_ref = f32[32,8,128]{2,1,0:T(8,128)S(1)} all-to-all(f32[32,8,128]{2,1,0:T(8,128)S(1)} %spread.1), channel_id=1, replica_groups=mesh['member'=4,'space'=8] {'member','space'}, dimensions={0} | all-to-all | bytes 262144 | tf_op jit(solution)/shard_map/all_to_all | solution.py:428
  62.7 0.0 copy-done
  62.7 5.6 %update.1 = (f32[1024,128]{1,0:T(8,128)}, f32[128,128]{1,0:T(8,128)}) custom-call(f32[32,8,128]{2,1,0:T(8,128)S(1)} %all_to_all.23.sums_ref, f32[1024,128]{1,0:T(8,128)S(1)} %bitcast.23, f32[128,128]{1,0:T(8,128)S(1)} %bitcast.25), custom_call_target="tpu_custom_call" | custom-call | tf_op jit(solution)/shard_map/update/pallas_call | solution.py:123
  (1 shorter events, 0.0 us)
Async XLA Ops:
  42.5 20.1 %copy-start = (f32[128,2,4,128]{3,2,1,0:T(4,128)S(1)}, f32[128,2,4,128]{3,2,1,0:T(4,128)}, u32[]{:S(2)}) copy-start(f32[128,2,4,128]{3,2,1,0:T(4,128)} %param.6) | copy-start | bytes 1572868

commit v8 on v7

--- a/solution.py
+++ b/solution.py
@@ -185,7 +185,7 @@
             fn(j)
             return carry
 
-        lax.fori_loop(0, held, body, 0)
+        lax.fori_loop(0, held, body, 0, unroll=2 - held % 2)
 
     for ref in (p_ref, fy_ref):
         for edge in (0, TILE + held * nx * ny):
@@ -225,7 +225,8 @@
             fz = jnp.where(lane > 0, 2.0 / (e + pltpu.roll(e, 1, 1)), 0.0)
             fy_ref[at(j, x), :] = fy
             fz_ref[at(j, x), :] = fz
-            mid = (fy + pltpu.roll(fy, ny - 1, 0)) + (fz + pltpu.roll(fz, nz - 1, 1))
+            fz_up = jnp.where(lane < nz - 1, 2.0 / (e + pltpu.roll(e, nz - 1, 1)), 0.0)
+            mid = (fy + pltpu.roll(fy, ny - 1, 0)) + (fz + fz_up)
             ends = edge_y + edge_z
             if x == 0 or x == nx - 1:
                 ends = ends + 1.0
@@ -379,6 +380,7 @@
     lane = lax.broadcasted_iota(jnp.int32, (tile, members), 1)
     sub = lax.broadcasted_iota(jnp.int32, (tile, members), 0)
     blocks = members // tile
+    ones = (lane >= 0).astype(jnp.float32)
     left, right = [], []
     for k in range(blocks):
         own = (lane == sub + k * tile).astype(jnp.float32) * (members - 1.0)
@@ -393,7 +395,7 @@
         return jnp.broadcast_to(x[:, t : t + 1], wide)
 
     for k in range(blocks):
-        parts = [column(left[k], k * tile + t) for t in range(tile)] + [left[k], right[k]]
+        parts = [column(left[k], k * tile + t) * ones for t in range(tile)] + [left[k], right[k]]
         for t in range(tile):
             inverse = 1.0 / row(parts[t], t)
             factor = jnp.where(sub == t, 0.0, parts[t] * inverse)

time: 68.5 us -> 68.1 us (level)
  no operation moved by 1% of the time
where the time goes in v8:
time: 68.1 us; the launch traced here: 67.9 us
  blocking collectives  55.7 us (82%)
  Pallas kernels  10.8 us (16%)
  between operations  1.31 us (2%)
    all_to_all x4, blocking collectives, exchange(): return lax.all_to_all(x, AXES, split_axis=0, concat_axis=0, tiled=True)  55.7 us
    pallas_call x5, Pallas kernels, vmem_call(): pl.pallas_call(kernel, out_shape=out, in_specs=specs, out_specs=outs, scr...  10.8 us

profile of v8, /device:TPU:0, one launch (start us, length us, event | category | flops | bytes accessed | tf_op | source)
XLA Modules:
  0.0 67.9 jit_solution(2603598214396916739)
XLA Ops:
  1.3 1.1 %pack.1 = f32[32,41,1,128]{3,2,1,0:T(1,128)S(1)} custom-call(f32[32,32,1,128]{3,2,1,0:T(1,128)} %bitcast.22, f32[8,1,128]{2,1,0:T(1,128)} %bitcast.28, s32[1]{0:T(128)} %bitcast.19.obs_ref), custom_call_target="tpu_custom_call" | custom-call | tf_op jit(solution)/shard_map/pack/pallas_call | solution.py:123
  2.4 26.5 %all_to_all.20 = f32[1312,1,128]{2,1,0:T(1,128)S(1)} all-to-all(f32[1312,1,128]{2,1,0:T(1,128)S(1)} %bitcast.21), channel_id=1, replica_groups=mesh['member'=4,'space'=8] {'member','space'}, dimensions={0} | all-to-all | bytes 1343488 | tf_op jit(solution)/shard_map/all_to_all | solution.py:430
  28.9 3.9 %pressure.1 = (f32[128,128]{1,0:T(8,128)S(1)}, f32[128,128]{1,0:T(8,128)S(1)}, f32[1,128]{1,0:T(1,128)S(1)}) custom-call(f32[1312,128]{1,0:T(8,128)S(1)} %bitcast.20, f32[1,128]{1,0:T(1,128)} %bitcast.29, f32[128,128]{1,0:T(8,128)} %bitcast.27, f32[1,128]{1,0:T(1,128)} %bitcast.30), custom_call_target="tpu_custom_call" | custom-call | tf_op jit(solution)/shard_map/pressure/pallas_call | solution.py:123
  32.8 9.5 %all_to_all.21 = f32[128,1,128]{2,1,0:T(1,128)S(1)} all-to-all(f32[128,1,128]{2,1,0:T(1,128)S(1)} %bitcast.26), channel_id=1, replica_groups=mesh['member'=4,'space'=8] {'member','space'}, dimensions={0} | all-to-all | bytes 131072 | tf_op jit(solution)/shard_map/all_to_all | solution.py:430
  42.3 0.0 copy-start
  42.3 0.4 sums.1
  42.6 9.9 %all_to_all.22.parts_ref = f32[32,8,128]{2,1,0:T(8,128)S(1)} all-to-all(f32[32,8,128]{2,1,0:T(8,128)S(1)} %sums.1), channel_id=1, replica_groups=mesh['member'=4,'space'=8] {'member','space'}, dimensions={0} | all-to-all | bytes 262144 | tf_op jit(solution)/shard_map/all_to_all | solution.py:430
  52.6 9.9 %all_to_all.23.sums_ref = f32[32,8,128]{2,1,0:T(8,128)S(1)} all-to-all(f32[32,8,128]{2,1,0:T(8,128)S(1)} %spread.1), channel_id=1, replica_groups=mesh['member'=4,'space'=8] {'member','space'}, dimensions={0} | all-to-all | bytes 262144 | tf_op jit(solution)/shard_map/all_to_all | solution.py:430
  62.4 0.0 copy-done
  62.4 5.5 %update.1 = (f32[1024,128]{1,0:T(8,128)}, f32[128,128]{1,0:T(8,128)}) custom-call(f32[32,8,128]{2,1,0:T(8,128)S(1)} %all_to_all.23.sums_ref, f32[1024,128]{1,0:T(8,128)S(1)} %bitcast.23, f32[128,128]{1,0:T(8,128)S(1)} %bitcast.25), custom_call_target="tpu_custom_call" | custom-call | tf_op jit(solution)/shard_map/update/pallas_call | solution.py:123
  (1 shorter events, 0.0 us)
Async XLA Ops:
  42.3 20.1 %copy-start = (f32[128,2,4,128]{3,2,1,0:T(4,128)S(1)}, f32[128,2,4,128]{3,2,1,0:T(4,128)}, u32[]{:S(2)}) copy-start(f32[128,2,4,128]{3,2,1,0:T(4,128)} %param.6) | copy-start | bytes 1572868

commit v9 on v8

--- a/solution.py
+++ b/solution.py
@@ -140,9 +140,9 @@
     fields = pltpu.make_async_copy(field_ref, out_ref.at[:, pl.ds(0, cells)], sems.at[0])
     source = pltpu.make_async_copy(source_ref, block_ref, sems.at[1])
     rows = pltpu.make_async_copy(obs_ref, rows_ref, sems.at[2])
+    fields.start()
     rows.start()
     source.start()
-    fields.start()
     rows.wait()
     for o in range(n_obs):
         pick = jnp.full((1, 1, nz), rows_ref[o].astype(jnp.float32))
@@ -245,7 +245,9 @@
 
     def turn(j, ratio):
         for x in range(nx):
-            v = r_ref[at(j, x), :] + ratio * p_ref[at(j, x), :]
+            v = r_ref[at(j, x), :]
+            if ratio is not None:
+                v = v + ratio * p_ref[at(j, x), :]
             p_ref[at(j, x), :] = v
             f = fz_ref[at(j, x), :]
             q_ref[at(j, x), :] = f * pltpu.roll(v, 1, 1) + pltpu.roll(f * v, nz - 1, 1)
@@ -318,7 +320,7 @@
         return carry
 
     acc_ref[...] = jnp.zeros(acc_ref.shape, jnp.float32)
-    together(*[turn(j, acc_ref[member(j), :]) for j in ahead])
+    together(*[turn(j, None) for j in ahead])
     lax.fori_loop(0, ITERS - 1, one, 0)
     steps, dots = open_stage(), {}
     together(*[apply(j, dots) for j in behind])

time: 68.1 us -> 68.1 us (level)
  no operation moved by 1% of the time
where the time goes in v9:
time: 68.1 us; the launch traced here: 67.9 us
  blocking collectives  55.7 us (82%)
  Pallas kernels  10.8 us (16%)
  between operations  1.31 us (2%)
    all_to_all x4, blocking collectives, exchange(): return lax.all_to_all(x, AXES, split_axis=0, concat_axis=0, tiled=True)  55.7 us
    pallas_call x5, Pallas kernels, vmem_call(): pl.pallas_call(kernel, out_shape=out, in_specs=specs, out_specs=outs, scr...  10.8 us

profile of v9, /device:TPU:0, one launch (start us, length us, event | category | flops | bytes accessed | tf_op | source)
XLA Modules:
  0.0 67.9 jit_solution(1171526479716124945)
XLA Ops:
  1.3 1.1 %pack.1 = f32[32,41,1,128]{3,2,1,0:T(1,128)S(1)} custom-call(f32[32,32,1,128]{3,2,1,0:T(1,128)} %bitcast.22, f32[8,1,128]{2,1,0:T(1,128)} %bitcast.28, s32[1]{0:T(128)} %bitcast.19.obs_ref), custom_call_target="tpu_custom_call" | custom-call | tf_op jit(solution)/shard_map/pack/pallas_call | solution.py:123
  2.4 26.5 %all_to_all.20 = f32[1312,1,128]{2,1,0:T(1,128)S(1)} all-to-all(f32[1312,1,128]{2,1,0:T(1,128)S(1)} %bitcast.21), channel_id=1, replica_groups=mesh['member'=4,'space'=8] {'member','space'}, dimensions={0} | all-to-all | bytes 1343488 | tf_op jit(solution)/shard_map/all_to_all | solution.py:432
  28.9 3.9 %pressure.1 = (f32[128,128]{1,0:T(8,128)S(1)}, f32[128,128]{1,0:T(8,128)S(1)}, f32[1,128]{1,0:T(1,128)S(1)}) custom-call(f32[1312,128]{1,0:T(8,128)S(1)} %bitcast.20, f32[1,128]{1,0:T(1,128)} %bitcast.29, f32[128,128]{1,0:T(8,128)} %bitcast.27, f32[1,128]{1,0:T(1,128)} %bitcast.30), custom_call_target="tpu_custom_call" | custom-call | tf_op jit(solution)/shard_map/pressure/pallas_call | solution.py:123
  32.8 9.5 %all_to_all.21 = f32[128,1,128]{2,1,0:T(1,128)S(1)} all-to-all(f32[128,1,128]{2,1,0:T(1,128)S(1)} %bitcast.26), channel_id=1, replica_groups=mesh['member'=4,'space'=8] {'member','space'}, dimensions={0} | all-to-all | bytes 131072 | tf_op jit(solution)/shard_map/all_to_all | solution.py:432
  42.3 0.0 copy-start
  42.3 0.4 sums.1
  42.6 9.9 %all_to_all.22.parts_ref = f32[32,8,128]{2,1,0:T(8,128)S(1)} all-to-all(f32[32,8,128]{2,1,0:T(8,128)S(1)} %sums.1), channel_id=1, replica_groups=mesh['member'=4,'space'=8] {'member','space'}, dimensions={0} | all-to-all | bytes 262144 | tf_op jit(solution)/shard_map/all_to_all | solution.py:432
  52.5 9.9 %all_to_all.23.sums_ref = f32[32,8,128]{2,1,0:T(8,128)S(1)} all-to-all(f32[32,8,128]{2,1,0:T(8,128)S(1)} %spread.1), channel_id=1, replica_groups=mesh['member'=4,'space'=8] {'member','space'}, dimensions={0} | all-to-all | bytes 262144 | tf_op jit(solution)/shard_map/all_to_all | solution.py:432
  62.4 0.0 copy-done
  62.4 5.5 %update.1 = (f32[1024,128]{1,0:T(8,128)}, f32[128,128]{1,0:T(8,128)}) custom-call(f32[32,8,128]{2,1,0:T(8,128)S(1)} %all_to_all.23.sums_ref, f32[1024,128]{1,0:T(8,128)S(1)} %bitcast.23, f32[128,128]{1,0:T(8,128)S(1)} %bitcast.25), custom_call_target="tpu_custom_call" | custom-call | tf_op jit(solution)/shard_map/update/pallas_call | solution.py:123
  (1 shorter events, 0.0 us)
Async XLA Ops:
  42.3 20.1 %copy-start = (f32[128,2,4,128]{3,2,1,0:T(4,128)S(1)}, f32[128,2,4,128]{3,2,1,0:T(4,128)}, u32[]{:S(2)}) copy-start(f32[128,2,4,128]{3,2,1,0:T(4,128)} %param.6) | copy-start | bytes 1572868
